TPU v7x, 256 devices: a whole 4x4x8 slice. The times are simulated.
256 devices in a mesh: north: 8 (over y_hi, x), east: 32 (over z, y_lo, core).
Axes of the slice: x: 4, y: 4 (y_hi: 2, y_lo: 2; y = y_hi * 2 + y_lo), z: 8, core: 2. Of those that a mesh axis runs over, the one named last changes fastest.
Arguments:
- pair_rows: bfloat16 [768, 768, 128], P('north', 'east'), may hold values from -6 to 6
- in_gain: float32 [128], replicated, may hold values from 0.25 to 1.75
- left_weight: bfloat16 [128, 128], replicated, may hold values from -0.5 to 0.5
- right_weight: bfloat16 [128, 128], replicated, may hold values from -0.5 to 0.5
- left_gate: bfloat16 [128, 128], replicated, may hold values from -0.5 to 0.5
- right_gate: bfloat16 [128, 128], replicated, may hold values from -0.5 to 0.5
- mid_gain: float32 [128], replicated, may hold values from 0.25 to 1.75
- out_weight: bfloat16 [128, 128], replicated, may hold values from -0.5 to 0.5
- out_gate: bfloat16 [128, 128], replicated, may hold values from -0.5 to 0.5
Outputs:
- pair_change: bfloat16 [768, 768, 128], P('north', 'east')
All inputs are finite; a program needn't handle non-finite values.
Results may differ from a plain program's by a relative error of at most 0.012.
Values may be sent and summed in bfloat16 or wider, within the bound.
A program may use at most 128 MiB of HBM per device.

v0:
```python
import jax
import jax.numpy as jnp
from jax import lax
from jax.sharding import PartitionSpec as P


def scale_channels(values, channel_gain):
    centred = values - jnp.mean(values, axis=-1, keepdims=True)
    return (
        centred
        * lax.rsqrt(jnp.mean(centred * centred, axis=-1, keepdims=True) + 1e-05)
        * channel_gain
    )


def both_factors(pair_in, in_gain, left_weight, right_weight, left_gate, right_gate):
    ready = scale_channels(pair_in.astype(jnp.float32), in_gain).astype(jnp.bfloat16)
    ready = lax.optimization_barrier(ready)
    left = jnp.einsum("ijc,cd->ijd", ready, left_weight, preferred_element_type=jnp.float32)
    left = left * jax.nn.sigmoid(
        jnp.einsum("ijc,cd->ijd", ready, left_gate, preferred_element_type=jnp.float32)
    )
    right = jnp.einsum("ijc,cd->ijd", ready, right_weight, preferred_element_type=jnp.float32)
    right = right * jax.nn.sigmoid(
        jnp.einsum("ijc,cd->ijd", ready, right_gate, preferred_element_type=jnp.float32)
    )
    return (ready, left.astype(jnp.bfloat16), right.astype(jnp.bfloat16))


def to_pair(mixed, ready, mid_gain, out_weight, out_gate):
    scaled = scale_channels(mixed.astype(jnp.float32), mid_gain).astype(jnp.bfloat16)
    scaled = lax.optimization_barrier(scaled)
    gate = jax.nn.sigmoid(
        jnp.einsum("ijc,cd->ijd", ready, out_gate, preferred_element_type=jnp.float32)
    )
    return (
        jnp.einsum("ijd,dc->ijc", scaled, out_weight, preferred_element_type=jnp.float32) * gate
    ).astype(jnp.bfloat16)


def body(
    pair_rows,
    in_gain,
    left_weight,
    right_weight,
    left_gate,
    right_gate,
    mid_gain,
    out_weight,
    out_gate,
):
    ready, left, right = both_factors(
        pair_rows, in_gain, left_weight, right_weight, left_gate, right_gate
    )
    count = pair_rows.shape[0] * lax.axis_size("north")
    left_lines, right_lines = (
        lax.all_to_all(left, "north", split_axis=2, concat_axis=0, tiled=True),
        lax.all_to_all(right, "north", split_axis=2, concat_axis=0, tiled=True),
    )
    strip = jnp.einsum(
        "kid,kjd->ijd",
        lax.all_gather(left_lines, "east", axis=1, tiled=True),
        right_lines,
        preferred_element_type=jnp.float32,
    )
    strip = (strip * count ** (-0.5)).astype(jnp.bfloat16)
    mixed = lax.all_to_all(strip, "north", split_axis=0, concat_axis=2, tiled=True)
    return to_pair(mixed, ready, mid_gain, out_weight, out_gate)


def solution(mesh):
    placed = (P("north", "east", None), P(), P(), P(), P(), P(), P(), P(), P())
    return jax.shard_map(
        body, mesh=mesh, in_specs=placed, out_specs=P("north", "east", None), check_vma=False
    )
```

profile of v0, /device:TPU:8, one launch (start us, length us, event | category | flops | bytes accessed | tf_op | source)
XLA Modules:
  0.0 205.3 jit_solution(16106482152377002124)
XLA Ops:
  6.5 0.0 copy-start
  6.5 0.0 copy-start.1
  6.5 0.0 copy-start.7
  6.5 0.0 all-gather.2.cloned.1.call-start
  6.5 1.5 convert_reduce_fusion
  8.1 0.1 copy.48
  8.1 0.1 copy.49
  8.2 0.0 copy-done.1
  8.2 0.7 fusion.21
  8.9 0.1 copy.50
  9.0 0.1 copy.51
  9.1 0.0 copy-done.7
  9.1 0.8 fusion.23
  9.9 0.0 copy-done
  9.9 0.0 copy-start.2
  9.9 0.0 copy-start.4
  10.0 0.5 fusion.12
  10.4 0.3 copy-done.4
  10.7 0.4 fusion.17
  11.2 0.6 copy.55
  11.8 20.2 %all_to_all.45 = bf16[96,24,128]{0,1,2:T(8,128)(2,1)S(1)} all-to-all(bf16[96,24,128]{0,1,2:T(8,128)(2,1)S(1)} %copy.55), channel_id=1, replica_groups=mesh['north'=8,'east'=32] {'north'}, dimensions={2} | all-to-all | bytes 1179648 | tf_op jit(solution)/shard_map/all_to_all | solution.py:57
  32.0 0.5 copy.57
  32.5 0.0 copy-start.9
  32.5 1.5 all_to_all.40
  34.0 0.0 all-gather.2.cloned.1.call-update
  34.0 0.0 copy-done.9
  34.0 0.0 copy-start.5
  34.1 0.5 fusion.15
  34.5 0.0 copy-done.2
  34.5 0.3 copy-done.5
  34.8 0.4 fusion.16
  35.3 0.6 copy.52
  35.9 16.0 %all_to_all.46 = bf16[96,24,128]{0,1,2:T(8,128)(2,1)S(1)} all-to-all(bf16[96,24,128]{0,1,2:T(8,128)(2,1)S(1)} %copy.52), channel_id=1, replica_groups=mesh['north'=8,'east'=32] {'north'}, dimensions={2} | all-to-all | bytes 1179648 | tf_op jit(solution)/shard_map/all_to_all | solution.py:58
  51.8 0.5 copy.54
  52.3 0.6 all_to_all.36
  53.0 92.8 %all-gather.2.cloned.1.call-done = bf16[768,768,16]{0,1,2:T(8,128)(2,1)} async-done(((bf16[768,24,16]{0,1,2:T(8,128)(2,1)}), bf16[768,768,16]{0,1,2:T(8,128)(2,1)}) %all-gather.2.cloned.1.call-update) | async-done | bytes 18874384 | tf_op jit(solution)/shard_map/all_gather | solution.py:62
  145.8 12.2 %fusion.20 = bf16[768,24,16]{0,1,2:T(8,128)(2,1)} fusion(bf16[768,24,16]{0,1,2:T(8,128)(2,1)S(1)} %all_to_all.36, bf16[768,768,16]{0,1,2:T(8,128)(2,1)} %all-gather.2.cloned.1.call-done), kind=kOutput, calls=%fused_computation.32 | convolution fusion | flops 453574656 | bytes 20054016 | tf_op jit(solution)/shard_map/kid,kjd->ijd/dot_general | solution.py:60
  158.0 3.8 %copy.58 = bf16[768,24,16]{1,2,0:T(8,128)(2,1)S(1)} copy(bf16[768,24,16]{0,1,2:T(8,128)(2,1)} %fusion.20) | data formatting | bytes 1179648 | tf_op jit(solution)/shard_map/convert_element_type | solution.py:66
  161.8 4.6 %reshape.41 = bf16[8,2,18432]{2,1,0:T(2,128)(2,1)} reshape(bf16[768,16,24]{2,1,0:T(8,128)(2,1)S(1)} %bitcast.62) | data formatting | bytes 1179648
  166.4 0.0 copy-start.3
  166.4 0.0 copy-start.10
  166.4 5.1 %all-to-all-start.2 = ((bf16[8,2,18432]{2,1,0:T(2,128)(2,1)}), bf16[8,2,18432]{2,1,0:T(2,128)(2,1)S(1)}, u32[]{:S(2)}, u32[]{:S(2)}) async-start(bf16[8,2,18432]{2,1,0:T(2,128)(2,1)} %reshape.41), calls=%async_computation.2 | async-start | bytes 1179648 | tf_op jit(solution)/shard_map/all_to_all | solution.py:67
  171.5 0.0 copy-done.3
  171.5 0.0 copy-done.10
  171.5 1.5 fusion.9
  173.0 11.2 %all-to-all-done.2 = bf16[8,2,18432]{2,1,0:T(2,128)(2,1)S(1)} async-done(((bf16[8,2,18432]{2,1,0:T(2,128)(2,1)}), bf16[8,2,18432]{2,1,0:T(2,128)(2,1)S(1)}, u32[]{:S(2)}, u32[]{:S(2)}) %all-to-all-start.2) | async-done | bytes 589856 | tf_op jit(solution)/shard_map/all_to_all | solution.py:67
  184.2 5.3 %reshape.42 = bf16[768,16,24]{2,1,0:T(8,128)(2,1)} reshape(bf16[8,2,18432]{2,1,0:T(2,128)(2,1)S(1)} %all-to-all-done.2) | data formatting | bytes 1179648
  189.5 4.6 %copy.59 = f32[8,96,24,16]{1,3,0,2:T(8,128)S(1)} copy(bf16[8,96,24,16]{2,3,1,0:T(8,128)(2,1)} %bitcast.63) | data formatting | bytes 1769472 | tf_op jit(solution)/shard_map/convert_element_type | solution.py:31
  194.1 0.1 bitcast_reduce_fusion
  194.2 0.0 copy-start.8
  194.2 0.2 fusion.4
  194.5 0.4 copy-done.8
  194.9 0.3 fusion.2
  195.2 0.0 copy-start.6
  195.2 0.4 copy.60
  195.6 0.4 copy-done.6
  196.0 2.5 %fusion.18 = bf16[96,24,128]{2,1,0:T(8,128)(2,1)} fusion(f32[96,24,128]{2,1,0:T(8,128)} %fusion.9, bf16[96,24,128]{2,1,0:T(8,128)(2,1)S(1)} %copy.60, bf16[128,128]{1,0:T(8,128)(2,1)S(1)} %copy-done.6), kind=kOutput, calls=%fused_computation.30 | convolution fusion | flops 76087296 | bytes 2392064 | tf_op jit(solution)/shard_map/ijd,dc->ijc/dot_general | solution.py:37
  (4 shorter events, 0.0 us)
Async XLA Ops:
  6.5 3.4 %copy-start = (bf16[128,128]{1,0:T(8,128)(2,1)S(1)}, bf16[128,128]{1,0:T(8,128)(2,1)}, u32[]{:S(2)}) copy-start(bf16[128,128]{1,0:T(8,128)(2,1)} %param.13) | copy-start | bytes 98308
  6.5 1.7 copy-start.1
  6.5 2.6 %copy-start.7 = (f32[128]{0:T(128)S(1)}, f32[128]{0:T(128)}, u32[]{:S(2)}) copy-start(f32[128]{0:T(128)} %param.10) | copy-start | bytes 1540
  6.5 139.2 %all-gather.2.cloned.1.call-start = ((), (), s32[]{:S(2)}) async-start(), calls=%async_computation.3 | async-start | bytes 19464192 | tf_op jit(solution)/shard_map/all_gather | solution.py:62
  9.9 24.6 %copy-start.2 = (bf16[96,24,128]{2,1,0:T(8,128)(2,1)}, bf16[96,24,128]{2,1,0:T(8,128)(2,1)S(1)}, u32[]{:S(2)}) copy-start(bf16[96,24,128]{2,1,0:T(8,128)(2,1)S(1)} %fusion.23) | copy-start | bytes 1769476
  9.9 0.8 copy-start.4
  32.5 1.5 copy-start.9
  34.0 0.8 copy-start.5
  166.4 5.1 %copy-start.3 = (bf16[96,24,128]{2,1,0:T(8,128)(2,1)S(1)}, bf16[96,24,128]{2,1,0:T(8,128)(2,1)}, u32[]{:S(2)}) copy-start(bf16[96,24,128]{2,1,0:T(8,128)(2,1)} %copy-done.2) | copy-start | bytes 1769476
  166.4 5.1 %copy-start.10 = (bf16[128,128]{1,0:T(8,128)(2,1)S(1)}, bf16[128,128]{1,0:T(8,128)(2,1)}, u32[]{:S(2)}) copy-start(bf16[128,128]{1,0:T(8,128)(2,1)} %param.17) | copy-start | bytes 98308
  166.4 17.8 %all-to-all-start.2 = ((bf16[8,2,18432]{2,1,0:T(2,128)(2,1)}), bf16[8,2,18432]{2,1,0:T(2,128)(2,1)S(1)}, u32[]{:S(2)}, u32[]{:S(2)}) async-start(bf16[8,2,18432]{2,1,0:T(2,128)(2,1)} %reshape.41), calls=%async_computation.2 | async-start | bytes 1179648 | tf_op jit(solution)/shard_map/all_to_all | solution.py:67
  194.2 0.7 copy-start.8
  195.2 0.8 copy-start.6
Sparse Core Ops, SparseCore 0:
  34.2 111.5 all-gather.1
where the time goes:
time: 208 us; the launch traced here: 205 us
  waiting for transfers between devices  104 us (50%)
  blocking collectives  36.2 us (17%)
  local copies, waits for them, and re-layouts  24.7 us (12%)
  matrix products  18.1 us (9%)
  between operations  13.7 us (7%)
  starting transfers between devices  5.07 us (2%)
  other arithmetic  3.72 us (2%)
    all_gather x1, waiting for transfers between devices, body(): lax.all_gather(left_lines, 'east', axis=1, tiled=True)  92.8 us
    all_to_all x1, blocking collectives, body(): lax.all_to_all(left, 'north', split_axis=2, concat_axis=0, tiled=True)  20.2 us
    all_to_all x1, blocking collectives, body(): lax.all_to_all(right, 'north', split_axis=2, concat_axis=0, tiled=True)  16 us
    dot_general x1, matrix products, body(): jnp.einsum('kid,kjd->ijd', lax.all_gather(left_lines, 'east', axis=1, til...  12.2 us
    unnamed x24, local copies, waits for them, and re-layouts  11.3 us
    all_to_all x1, waiting for transfers between devices, body(): lax.all_to_all(strip, 'north', split_axis=0, concat_axis=2, tiled=True)  11.2 us
    all_to_all x1, starting transfers between devices, body(): lax.all_to_all(strip, 'north', split_axis=0, concat_axis=2, tiled=True)  5.07 us
    convert_element_type x1, local copies, waits for them, and re-layouts, to_pair(): mixed.astype(jnp.float32)  4.56 us
  transfers between devices with their start and end apart: 2, of which 2 were waited for; matrix products, arithmetic and copies ran while one was open for 2% of the time, Pallas kernels for 0%

commit v1 on v0

v1 whole, which is shorter than its diff:
```python
import jax
import jax.numpy as jnp
from jax import lax
from jax.experimental import pallas as pl
from jax.experimental.pallas import tpu as pltpu
from jax.sharding import PartitionSpec as P

MESH = pl.DeviceIdType.MESH
F32, BF16 = jnp.float32, jnp.bfloat16

RES, WIDTH = 768, 128
NORTH, EAST, CHIPS = 8, 32, 16
KB, IB = RES // NORTH, RES // EAST
ROWS = KB * IB
GROUP = WIDTH // NORTH
SPAN = 4 * KB
STEPS = ROWS // SPAN
HALF = RES // 2


def turn(values, amount):
    amount = amount % SPAN
    return values if amount == 0 else pltpu.roll(values, amount, axis=1)


def regroup(parts):
    lane = lax.broadcasted_iota(jnp.int32, parts[0].shape, 1)
    out = []
    for b in range(4):
        row = turn(parts[0], -KB * b)
        for a in range(1, 4):
            row = jnp.where(lane >= KB * a, turn(parts[a], KB * (a - b)), row)
        out.append(row)
    return out


def nt(a, b):
    return lax.dot_general(a, b, (((1,), (1,)), ((), ())), preferred_element_type=F32)


def kernel(
    x_ref, in_gain, lw, rw, lg, rg, mid_gain, ow, og, out_ref,
    flat, ready, wt, send1, got1, mid, send2, left, right, sums, got3, send4, got4, gate, gain_col,
    s1, r1, s2l, r2l, s2r, r2r, sf, rf, s3, r3, s4, r4,
):
    n = lax.axis_index("north")
    e = lax.axis_index("east")
    zy, c = e // 2, lax.rem(e, 2)
    half = zy // 8

    def remote(src, dst, ssem, rsem, where):
        return pltpu.make_async_remote_copy(
            src_ref=src, dst_ref=dst, send_sem=ssem, recv_sem=rsem,
            device_id=where, device_id_type=MESH,
        )

    barrier = pltpu.get_barrier_semaphore()
    for s in range(1, NORTH):
        pl.semaphore_signal(
            barrier, inc=1, device_id={"north": lax.rem(n + s, NORTH)}, device_id_type=MESH
        )
    for s in range(1, EAST):
        pl.semaphore_signal(
            barrier, inc=1, device_id={"east": lax.rem(e + s, EAST)}, device_id_type=MESH
        )

    @pl.loop(0, 4)
    def _(b):
        rows = pl.ds(b * (ROWS // 4), ROWS // 4)
        v = x_ref[rows, :].astype(F32)
        v = v - jnp.mean(v, axis=-1, keepdims=True)
        v = v * lax.rsqrt(jnp.mean(v * v, axis=-1, keepdims=True) + 1e-05) * in_gain[...]
        flat[rows, :] = v

    for i in range(IB):
        ready[i * KB : (i + 1) * KB, :] = flat[pl.ds(i, KB, stride=IB), :].astype(BF16)

    for p, w in enumerate((lw, lg, rw, rg)):
        wt[p * WIDTH : (p + 1) * WIDTH, :] = w[...].astype(F32).T.astype(BF16)
    gain_col[...] = jnp.broadcast_to(mid_gain[...], (WIDTH, WIDTH)).T

    hop1 = [[], []]
    for a in range(2):

        @pl.loop(0, STEPS)
        def _(g, a=a):
            cols = pl.ds(pl.multiple_of(g * SPAN, SPAN), SPAN)
            both = nt(wt[2 * a * WIDTH : 2 * (a + 1) * WIDTH, :], ready[cols, :])
            send1[a, :, cols] = (both[:WIDTH] * jax.nn.sigmoid(both[WIDTH:])).astype(BF16)

        if a == 0:
            pl.semaphore_wait(barrier, NORTH + EAST - 2)
        for s in range(1, NORTH):
            to = lax.rem(n + s, NORTH)
            copy = remote(
                send1.at[a, pl.ds(pl.multiple_of(to * GROUP, GROUP), GROUP), :],
                got1.at[a, n],
                s1.at[a, s], r1.at[a, s], {"north": to},
            )
            copy.start()
            hop1[a].append(copy)
        got1[a, n] = send1[a, pl.ds(pl.multiple_of(n * GROUP, GROUP), GROUP), :]

    def spread(a):
        @pl.loop(0, STEPS)
        def _(g):
            cols = pl.ds(pl.multiple_of(g * SPAN, SPAN), SPAN)
            for h in range(2):
                parts = [got1[a, 4 * h + q, :, cols].astype(F32) for q in range(4)]
                for b, row in enumerate(regroup(parts)):
                    for u in range(3):
                        mid[3 * h + u, pl.ds(4 * g + b, GROUP, stride=IB), :] = row[
                            :, u * 128 : (u + 1) * 128
                        ]

        @pl.loop(0, CHIPS)
        def _(d):
            for t in range(6):
                send2[a, d, :, t * 128 : (t + 1) * 128] = mid[
                    t, pl.ds(pl.multiple_of(d * IB, IB), IB), :
                ].astype(BF16)

    for copy in hop1[0]:
        copy.wait_recv()
    spread(0)
    lrow = pl.multiple_of((lax.rem(zy, 8) * 2 + c) * IB, IB)
    lsrc = lax.rem(zy, 8) * 2 + c
    hop2l = []
    for s in range(1, CHIPS):
        to = lax.rem(zy + s, CHIPS)
        copy = remote(
            send2.at[0, to], left.at[pl.ds(lrow, IB), :],
            s2l.at[s], r2l.at[lsrc], {"east": to * 2 + half},
        )
        copy.start()
        hop2l.append(copy)

    own_l = remote(
        send2.at[0, zy], left.at[pl.ds(lrow, IB), :], s2l.at[0], r2l.at[lsrc], {"east": zy * 2 + half}
    )

    @pl.when(c != half)
    def _():
        own_l.start()

    @pl.when(c == half)
    def _():
        left[pl.ds(lrow, IB), :] = send2[0, zy]

    for copy in hop1[1]:
        copy.wait_recv()
    spread(1)
    hop2r = []
    rrow = pl.multiple_of(e * IB, IB)
    partner = {"east": zy * 2 + 1 - c}
    for s in range(1, CHIPS):
        to = lax.rem(zy + s, CHIPS)
        copy = remote(
            send2.at[1, to], right.at[pl.ds(rrow, IB), :],
            s2r.at[s], r2r.at[s], {"east": to * 2 + c},
        )
        copy.start()
        hop2r.append(copy)
    shared = [
        remote(send2.at[1, zy], right.at[pl.ds(rrow, IB), :], sf.at[0], rf.at[0], partner)
    ]
    shared[0].start()
    right[pl.ds(rrow, IB), :] = send2[1, zy]

    @pl.loop(0, STEPS)
    def _(g):
        rows = pl.ds(pl.multiple_of(g * SPAN, SPAN), SPAN)
        gate[rows, :] = jax.nn.sigmoid(
            jnp.dot(ready[rows, :], og[...], preferred_element_type=F32)
        )

    for s in range(1, CHIPS):
        hop2r[s - 1].wait_recv()
        origin = lax.rem(zy + CHIPS - s, CHIPS) * 2 + c
        rows = pl.ds(pl.multiple_of(origin * IB, IB), IB)
        copy = remote(right.at[rows, :], right.at[rows, :], sf.at[s], rf.at[s], partner)
        copy.start()
        shared.append(copy)

    for p in range(CHIPS):

        @pl.when(jnp.logical_not((zy // 8 == c) & (lsrc == p)))
        def _(p=p):
            remote(
                send2.at[0, 0], left.at[pl.ds(p * IB, IB), :], s2l.at[0], r2l.at[p], partner
            ).wait_recv()

    for copy in shared:
        copy.wait_recv()

    hop3 = []
    quarter = RES // 4
    for t in range(4):
        at = lax.rem(zy // 4 + t, 4)
        rows = pl.ds(pl.multiple_of(at * quarter, quarter), quarter)
        sums[rows, :] = (nt(right[rows, :], left[...]) * RES ** (-0.5)).astype(BF16)
        for p in range(EAST // 4):
            to = at * (EAST // 4) + p
            block = sums.at[pl.ds(pl.multiple_of(to * IB, IB), IB), :]
            copy = remote(
                block, got3.at[zy, :, pl.ds(pl.multiple_of(c * HALF, HALF), HALF)],
                s3.at[t * (EAST // 4) + p], r3.at[e], {"east": to},
            )
            hop3.append((copy, to))

            @pl.when(to != e)
            def _(copy=copy):
                copy.start()

    mine = sums[pl.ds(pl.multiple_of(e * IB, IB), IB), :]

    @pl.when(c == 0)
    def _():
        got3[zy, :, :HALF] = mine

    @pl.when(c == 1)
    def _():
        got3[zy, :, HALF:] = mine

    hop4 = []
    for h in range(2):
        for p in range(CHIPS):
            @pl.when(jnp.logical_not((zy == p) & (c == h)))
            def _(p=p, h=h):
                remote(
                    sums.at[pl.ds(0, IB), :], got3.at[p, :, pl.ds(h * HALF, HALF)],
                    s3.at[0], r3.at[2 * p + h], partner,
                ).wait_recv()

        @pl.loop(0, CHIPS)
        def _(d, h=h):
            for u in range(3):
                t = 3 * h + u
                mid[t, pl.ds(pl.multiple_of(d * IB, IB), IB), :] = got3[
                    d, :, t * 128 : (t + 1) * 128
                ].astype(F32)

        @pl.loop(0, STEPS)
        def _(g, h=h):
            cols = pl.ds(pl.multiple_of(g * SPAN, SPAN), SPAN)
            parts = [
                jnp.concatenate(
                    [mid[3 * h + u, pl.ds(4 * g + b, GROUP, stride=IB), :] for u in range(3)], axis=1
                )
                for b in range(4)
            ]
            for q, row in enumerate(regroup(parts)):
                send4[4 * h + q, :, cols] = row.astype(BF16)

        for q in range(4):
            to = 4 * h + q
            copy = remote(
                send4.at[to], got4.at[pl.ds(pl.multiple_of(n * GROUP, GROUP), GROUP), :],
                s4.at[to], r4.at[n], {"north": to},
            )
            hop4.append(copy)

            @pl.when(to != n)
            def _(copy=copy):
                copy.start()

    got4[pl.ds(pl.multiple_of(n * GROUP, GROUP), GROUP), :] = send4[n]
    for p in range(NORTH):

        @pl.when(p != n)
        def _(p=p):
            remote(
                send4.at[0], got4.at[pl.ds(p * GROUP, GROUP), :], s4.at[0], r4.at[p], partner
            ).wait_recv()

    @pl.loop(0, STEPS)
    def _(g):
        cols = pl.ds(pl.multiple_of(g * SPAN, SPAN), SPAN)
        v = got4[:, cols].astype(F32)
        v = v - jnp.mean(v, axis=0, keepdims=True)
        v = v * lax.rsqrt(jnp.mean(v * v, axis=0, keepdims=True) + 1e-05)
        gains = jnp.concatenate([gain_col[...]] * 3, axis=1)
        v = (v * gains).astype(BF16)
        y = lax.dot_general(v, ow[...], (((0,), (0,)), ((), ())), preferred_element_type=F32)
        y = y * gate[cols, :]
        for b in range(4):
            flat[pl.ds(4 * g + b, KB, stride=IB), :] = y[b * KB : (b + 1) * KB]

    @pl.loop(0, 4)
    def _(b):
        rows = pl.ds(b * (ROWS // 4), ROWS // 4)
        out_ref[rows, :] = flat[rows, :].astype(BF16)

    for copy in hop1[0] + hop1[1] + hop2l + hop2r + shared:
        copy.wait_send()

    @pl.when(c != half)
    def _():
        own_l.wait_send()

    for copy, to in hop3:

        @pl.when(to != e)
        def _(copy=copy):
            copy.wait_send()

    for to, copy in enumerate(hop4):

        @pl.when(to != n)
        def _(copy=copy):
            copy.wait_send()


def body(pair_rows, in_gain, left_weight, right_weight, left_gate, right_gate, mid_gain, out_weight, out_gate):
    dma = pltpu.SemaphoreType.DMA
    vmem = pltpu.VMEM
    out = pl.pallas_call(
        kernel,
        out_shape=jax.ShapeDtypeStruct((ROWS, WIDTH), BF16),
        in_specs=[pl.BlockSpec(memory_space=vmem)] * 9,
        out_specs=pl.BlockSpec(memory_space=vmem),
        scratch_shapes=[
            vmem((ROWS, WIDTH), F32),
            vmem((ROWS, WIDTH), BF16),
            vmem((4 * WIDTH, WIDTH), BF16),
            vmem((2, WIDTH, ROWS), BF16),
            vmem((2, NORTH, GROUP, ROWS), BF16),
            vmem((6, GROUP * IB, 128), F32),
            vmem((2, CHIPS, IB, RES), BF16),
            vmem((HALF, RES), BF16),
            vmem((RES, RES), BF16),
            vmem((RES, HALF), BF16),
            vmem((CHIPS, IB, RES), BF16),
            vmem((NORTH, GROUP, ROWS), BF16),
            vmem((WIDTH, ROWS), BF16),
            vmem((ROWS, WIDTH), F32),
            vmem((WIDTH, WIDTH), F32),
            dma((2, NORTH)), dma((2, NORTH)),
            dma((CHIPS,)), dma((CHIPS,)),
            dma((CHIPS,)), dma((CHIPS,)),
            dma((CHIPS,)), dma((CHIPS,)),
            dma((EAST,)), dma((EAST,)),
            dma((NORTH,)), dma((NORTH,)),
        ],
        compiler_params=pltpu.CompilerParams(
            collective_id=0, has_side_effects=True, vmem_limit_bytes=60 * 2**20
        ),
        name="triangle",
    )(
        pair_rows.reshape(ROWS, WIDTH), in_gain.reshape(1, WIDTH), left_weight, right_weight,
        left_gate, right_gate, mid_gain.reshape(1, WIDTH), out_weight, out_gate,
    )
    return out.reshape(KB, IB, WIDTH)


def solution(mesh):
    placed = (P("north", "east", None), P(), P(), P(), P(), P(), P(), P(), P())
    return jax.shard_map(
        body, mesh=mesh, in_specs=placed, out_specs=P("north", "east", None), check_vma=False
    )
```

time: 208 us -> 82.5 us (0.40)
  the two profiles are of different devices: /device:TPU:8 before, /device:TPU:29 now
where the time goes in v1:
time: 82.5 us; the launch traced here: 82.3 us
  Pallas kernels  80.4 us (97%)
  local copies, waits for them, and re-layouts  1.94 us (2%)
    pallas_call x1, Pallas kernels, body(): pl.pallas_call(kernel, out_shape=jax.ShapeDtypeStruct((ROWS, WIDTH), BF16...  80.4 us
    unnamed x1, local copies, waits for them, and re-layouts  1.94 us

profile of v1, /device:TPU:29, one launch (start us, length us, event | category | flops | bytes accessed | tf_op | source)
XLA Modules:
  0.0 82.3 jit_solution(12260961576629600467)
XLA Ops:
  0.0 80.4 %triangle.1 = bf16[2304,128]{1,0:T(8,128)(2,1)} custom-call(bf16[2304,128]{1,0:T(8,128)(2,1)} %bitcast.5, f32[1,128]{1,0:T(1,128)} %bitcast.6, bf16[128,128]{1,0:T(8,128)(2,1)} %lw.1, bf16[128,128]{1,0:T(8,128)(2,1)} %rw.1, bf16[128,128]{1,0:T(8,128)(2,1)} %lg.1, bf16[128,128]{1,0:T(8,128)(2,1)} %rg.1, f32[1,128]{1,0:T(1,128)} %bitcast.7, ...), custom_call_target="tpu_custom_call" | custom-call | tf_op jit(solution)/shard_map/triangle/pallas_call | solution.py:317
  80.4 1.9 %copy.11 = bf16[96,24,128]{2,1,0:T(8,128)(2,1)} copy(bf16[96,24,128]{2,1,0:T(8,128)(2,1)} %bitcast.4) | data formatting | bytes 1179648

commit v2 on v0

v2 whole, which is shorter than its diff:
```python
import jax
import jax.numpy as jnp
from jax import lax
from jax.experimental import pallas as pl
from jax.experimental.pallas import tpu as pltpu
from jax.sharding import PartitionSpec as P

MESH = pl.DeviceIdType.MESH
F32, BF16 = jnp.float32, jnp.bfloat16

RES, WIDTH = 768, 128
NORTH, EAST, PLANE, DEPTH = 8, 32, 16, 8
KB, IB = RES // NORTH, RES // EAST
ROWS = KB * IB
WAVES, WI = 3, 8
LANES = WI * KB
SPAN = 4 * KB
HALF = RES // 2
PIECE = 2 * WI
SIDE = DEPTH * PIECE

STANDS = [y * 48 + c * 24 + w * WI for c in range(2) for w in range(WAVES) for y in range(2)]


def turn(values, amount):
    amount = amount % SPAN
    return values if amount == 0 else pltpu.roll(values, amount, axis=1)


def regroup(parts):
    lane = lax.broadcasted_iota(jnp.int32, parts[0].shape, 1)
    out = []
    for b in range(4):
        row = turn(parts[0], -KB * b)
        for a in range(1, 4):
            row = jnp.where(lane >= KB * a, turn(parts[a], KB * (a - b)), row)
        out.append(row)
    return out


def nt(a, b):
    return lax.dot_general(a, b, (((1,), (1,)), ((), ())), preferred_element_type=F32)


def remote(src, dst, ssem, rsem, where):
    return pltpu.make_async_remote_copy(
        src_ref=src, dst_ref=dst, send_sem=ssem, recv_sem=rsem,
        device_id=where, device_id_type=MESH,
    )


def kernel(
    x_ref, in_gain, lw, rw, lg, rg, mid_gain, ow, og, out_ref,
    flat, ready, wt, send1, got1, mid, send2, left, right, sums, got3, send4, got4, gate, gain_col,
    s1, r1, s2, r2, sf, rf, s3, r3, s4, r4,
):
    n = lax.axis_index("north")
    e = lax.axis_index("east")
    z, y, c = e // 4, lax.rem(e // 2, 2), lax.rem(e, 2)
    plane = n * 2 + y
    half = z // 4

    def on_plane(p):
        return (p // 2, (z * 2 + lax.rem(p, 2)) * 2 + c)

    def on_line(to_z, to_c):
        return (n, (to_z * 2 + y) * 2 + to_c)

    partner = on_line(z, 1 - c)

    with jax.named_scope("signal"):
        barrier = pltpu.get_barrier_semaphore()
        for s in range(1, 16):
            t = lax.rem(z * 2 + c + s, 16)
            for where in (on_plane(lax.rem(plane + s, PLANE)), on_line(t // 2, lax.rem(t, 2))):
                pl.semaphore_signal(barrier, inc=1, device_id=where, device_id_type=MESH)

    with jax.named_scope("norm"):

        @pl.loop(0, 4)
        def _(b):
            rows = pl.ds(b * (ROWS // 4), ROWS // 4)
            v = x_ref[rows, :].astype(F32)
            v = v - jnp.mean(v, axis=-1, keepdims=True)
            v = v * lax.rsqrt(jnp.mean(v * v, axis=-1, keepdims=True) + 1e-05) * in_gain[...]
            flat[rows, :] = v

    with jax.named_scope("perm"):
        for i in range(IB):
            line = [flat[pl.ds(k * IB + i, WI, stride=IB), :] for k in STANDS]
            ready[i * KB : (i + 1) * KB, :] = jnp.concatenate(line, axis=0).astype(BF16)
        for p, w in enumerate((lw, lg, rw, rg)):
            wt[p * WIDTH : (p + 1) * WIDTH, :] = w[...].astype(F32).T.astype(BF16)
        gain_col[...] = jnp.broadcast_to(mid_gain[...], (WIDTH, WIDTH)).T

    def project(a, w):
        for g in range(2):
            rows = ready[w * LANES + g * SPAN : w * LANES + (g + 1) * SPAN, :]
            both = nt(wt[2 * a * WIDTH : 2 * (a + 1) * WIDTH, :], rows)
            both = both[:WIDTH] * jax.nn.sigmoid(both[WIDTH:])
            send1[a, w, :, :, g * SPAN : (g + 1) * SPAN] = both.reshape(PLANE, 8, SPAN).astype(BF16)

    def across(a, w):
        for s in range(1, PLANE):
            to = lax.rem(plane + s, PLANE)
            remote(
                send1.at[a, w, to], got1.at[a, w, plane], s1.at[a, w], r1.at[a, w], on_plane(to)
            ).start()
        got1[a, w, plane] = send1[a, w, plane]

    def spread(a, w):
        rest = got1.at[a, w, pl.ds(0, PLANE - 1)]
        with jax.named_scope(f"wait1#{a}{w}"):
            remote(rest, rest, s1.at[a, w], r1.at[a, w], partner).wait_recv()
        with jax.named_scope(f"spread#{a}{w}"):
            for yy in range(2):
                for g in range(2):
                    for h in range(2):
                        parts = [
                            got1[a, w, (4 * h + q) * 2 + yy, :, g * SPAN : (g + 1) * SPAN].astype(F32)
                            for q in range(4)
                        ]
                        for b, row in enumerate(regroup(parts)):
                            for u in range(3):
                                at = pl.ds(yy * WI + 4 * g + b, DEPTH, stride=PIECE)
                                mid[3 * h + u, at, :] = row[:, u * 128 : (u + 1) * 128]
            for d in range(DEPTH):
                for t in range(6):
                    send2[a, w, d, :, t * 128 : (t + 1) * 128] = mid[
                        t, d * PIECE : (d + 1) * PIECE, :
                    ].astype(BF16)

    def left_at(w):
        return pl.ds(pl.multiple_of(lax.rem(z, 4) * KB + c * 48 + w * PIECE, PIECE), PIECE)

    right_at = pl.ds(pl.multiple_of(c * SIDE + z * PIECE, PIECE), PIECE)

    def along(a, w):
        for s in (1, 7, 2, 6, 3, 5, 4):
            to = lax.rem(z + s, DEPTH)
            if a == 0:
                dst, where = left.at[left_at(w), :], on_line(to, half)
            else:
                dst, where = right.at[w, right_at, :], on_line(to, c)
            remote(send2.at[a, w, to], dst, s2.at[a, w], r2.at[a, w], where).start()
        if a == 1:
            right[w, right_at, :] = send2[1, w, z]
        else:

            @pl.when(c == half)
            def _():
                left[left_at(w), :] = send2[0, w, z]

            @pl.when(c != half)
            def _():
                remote(
                    send2.at[0, w, z], left.at[left_at(w), :], s2.at[0, w], r2.at[0, w], partner
                ).start()

    with jax.named_scope("proj"):
        for a in range(2):
            for w in range(WAVES):
                project(a, w)
                if a == 0 and w == 0:
                    with jax.named_scope("barrier"):
                        pl.semaphore_wait(barrier, 30)
                across(a, w)

    for a in range(2):
        for w in range(WAVES):
            spread(a, w)
            with jax.named_scope(f"along#{a}{w}"):
                along(a, w)

    with jax.named_scope("gate"):

        @pl.loop(0, ROWS // SPAN)
        def _(g):
            rows = pl.ds(pl.multiple_of(g * SPAN, SPAN), SPAN)
            gate[rows, :] = jax.nn.sigmoid(
                jnp.dot(ready[rows, :], og[...], preferred_element_type=F32)
            )

    def share(w):
        mine = right.at[w, pl.ds(pl.multiple_of(c * SIDE, SIDE), SIDE), :]
        return remote(mine, mine, sf.at[w], rf.at[w], partner)

    def multiply(w):
        with jax.named_scope(f"wait2#{w}"):
            some = send2.at[1, w, pl.ds(0, DEPTH - 1)]
            remote(some, some, s2.at[1, w], r2.at[1, w], partner).wait_recv()
            share(w).start()
        if w == 0:
            with jax.named_scope("waitleft"):
                for ww in range(WAVES):
                    for count in (DEPTH, DEPTH - 1):

                        @pl.when((c == half) if count == DEPTH - 1 else (c != half))
                        def _(ww=ww, count=count):
                            some = send2.at[0, ww, pl.ds(0, count)]
                            remote(some, some, s2.at[0, ww], r2.at[0, ww], partner).wait_recv()

        with jax.named_scope(f"waitshare#{w}"):
            share(w).wait_recv()
        with jax.named_scope(f"mm#{w}"):
            sums[w] = (nt(right[w], left[...]) * RES ** (-0.5)).astype(BF16)
            for s in range(1, 16):
                t = lax.rem(z * 2 + c + s, 16)
                to_z, to_c = t // 2, lax.rem(t, 2)
                at = pl.ds(pl.multiple_of(to_c * SIDE + to_z * PIECE, PIECE), PIECE)
                remote(
                    sums.at[w, at, :],
                    got3.at[w, z, :, pl.ds(pl.multiple_of(c * HALF, HALF), HALF)],
                    s3.at[w], r3.at[w], on_line(to_z, to_c),
                ).start()
            mine = sums[w, right_at, :]

            @pl.when(c == 0)
            def _():
                got3[w, z, :, :HALF] = mine

            @pl.when(c == 1)
            def _():
                got3[w, z, :, HALF:] = mine

    for w in range(WAVES):
        multiply(w)

    def gather(w):
        with jax.named_scope(f"wait3#{w}"):
            some = sums.at[w, pl.ds(0, 15 * PIECE), :]
            remote(some, some, s3.at[w], r3.at[w], partner).wait_recv()
        with jax.named_scope(f"gather#{w}"):
            for d in range(DEPTH):
                for t in range(6):
                    mid[t, d * PIECE : (d + 1) * PIECE, :] = got3[
                        w, d, :, t * 128 : (t + 1) * 128
                    ].astype(F32)
            for yy in range(2):
                for g in range(2):
                    for h in range(2):
                        parts = [
                            jnp.concatenate(
                                [
                                    mid[3 * h + u, pl.ds(yy * WI + 4 * g + b, DEPTH, stride=PIECE), :]
                                    for u in range(3)
                                ],
                                axis=1,
                            )
                            for b in range(4)
                        ]
                        for q, row in enumerate(regroup(parts)):
                            send4[w, (4 * h + q) * 2 + yy, :, g * SPAN : (g + 1) * SPAN] = row.astype(BF16)
            for s in range(1, PLANE):
                to = lax.rem(plane + s, PLANE)
                remote(send4.at[w, to], got4.at[w, plane], s4.at[w], r4.at[w], on_plane(to)).start()
            got4[w, plane] = send4[w, plane]

    def finish(w):
        with jax.named_scope(f"wait4#{w}"):
            rest = got4.at[w, pl.ds(0, PLANE - 1)]
            remote(rest, rest, s4.at[w], r4.at[w], partner).wait_recv()
        with jax.named_scope(f"finish#{w}"):
            gains = jnp.concatenate([gain_col[...]] * 3, axis=1)
            for g in range(2):
                v = got4[w, :, :, g * SPAN : (g + 1) * SPAN].astype(F32).reshape(WIDTH, SPAN)
                v = v - jnp.mean(v, axis=0, keepdims=True)
                v = v * lax.rsqrt(jnp.mean(v * v, axis=0, keepdims=True) + 1e-05)
                v = (v * gains).astype(BF16)
                out = lax.dot_general(v, ow[...], (((0,), (0,)), ((), ())), preferred_element_type=F32)
                out = out * gate[w * LANES + g * SPAN : w * LANES + (g + 1) * SPAN, :]
                for b in range(4):
                    for p, i in enumerate(STANDS):
                        flat[pl.ds(i * IB + w * WI + 4 * g + b, WI, stride=IB), :] = out[
                            b * KB + p * WI : b * KB + (p + 1) * WI
                        ]

    gather(0)
    gather(1)
    finish(0)
    gather(2)
    finish(1)
    finish(2)

    with jax.named_scope("store"):

        @pl.loop(0, 4)
        def _(b):
            rows = pl.ds(b * (ROWS // 4), ROWS // 4)
            out_ref[rows, :] = flat[rows, :].astype(BF16)

    def sent(ref, sem):
        remote(ref, ref, sem, r4.at[0], partner).wait_send()

    with jax.named_scope("sent"):
        for w in range(WAVES):
            for a in range(2):
                sent(send1.at[a, w, pl.ds(0, PLANE - 1)], s1.at[a, w])
            sent(send2.at[1, w, pl.ds(0, DEPTH - 1)], s2.at[1, w])
            for count in (DEPTH, DEPTH - 1):

                @pl.when((c == half) if count == DEPTH - 1 else (c != half))
                def _(w=w, count=count):
                    sent(send2.at[0, w, pl.ds(0, count)], s2.at[0, w])

            share(w).wait_send()
            sent(sums.at[w, pl.ds(0, 15 * PIECE), :], s3.at[w])
            sent(send4.at[w, pl.ds(0, PLANE - 1)], s4.at[w])


def body(pair_rows, in_gain, left_weight, right_weight, left_gate, right_gate, mid_gain, out_weight, out_gate):
    dma = pltpu.SemaphoreType.DMA
    vmem = pltpu.VMEM
    out = pl.pallas_call(
        kernel,
        out_shape=jax.ShapeDtypeStruct((ROWS, WIDTH), BF16),
        in_specs=[pl.BlockSpec(memory_space=vmem)] * 9,
        out_specs=pl.BlockSpec(memory_space=vmem),
        scratch_shapes=[
            vmem((ROWS, WIDTH), F32),
            vmem((ROWS, WIDTH), BF16),
            vmem((4 * WIDTH, WIDTH), BF16),
            vmem((2, WAVES, PLANE, 8, LANES), BF16),
            vmem((2, WAVES, PLANE, 8, LANES), BF16),
            vmem((6, DEPTH * PIECE, 128), F32),
            vmem((2, WAVES, DEPTH, PIECE, RES), BF16),
            vmem((HALF, RES), BF16),
            vmem((WAVES, 2 * SIDE, RES), BF16),
            vmem((WAVES, 2 * SIDE, HALF), BF16),
            vmem((WAVES, DEPTH, PIECE, RES), BF16),
            vmem((WAVES, PLANE, 8, LANES), BF16),
            vmem((WAVES, PLANE, 8, LANES), BF16),
            vmem((ROWS, WIDTH), F32),
            vmem((WIDTH, WIDTH), F32),
            dma((2, WAVES)), dma((2, WAVES)),
            dma((2, WAVES)), dma((2, WAVES)),
            dma((WAVES,)), dma((WAVES,)),
            dma((WAVES,)), dma((WAVES,)),
            dma((WAVES,)), dma((WAVES,)),
        ],
        compiler_params=pltpu.CompilerParams(
            collective_id=0, has_side_effects=True, vmem_limit_bytes=60 * 2**20
        ),
        name="triangle",
    )(
        pair_rows.reshape(ROWS, WIDTH), in_gain.reshape(1, WIDTH), left_weight, right_weight,
        left_gate, right_gate, mid_gain.reshape(1, WIDTH), out_weight, out_gate,
    )
    return out.reshape(KB, IB, WIDTH)


def solution(mesh):
    placed = (P("north", "east", None), P(), P(), P(), P(), P(), P(), P(), P())
    return jax.shard_map(
        body, mesh=mesh, in_specs=placed, out_specs=P("north", "east", None), check_vma=False
    )
```

time: 208 us -> 66.7 us (0.32)
  waiting for transfers between devices: 104 us -> 0 us
  Pallas kernels: 0 us -> 63.7 us
  blocking collectives: 36.2 us -> 0 us
  local copies, waits for them, and re-layouts: 24.7 us -> 1.94 us
  matrix products: 18.1 us -> 0 us
  between operations: 13.7 us -> 0.01 us
  starting transfers between devices: 5.07 us -> 0 us
  other arithmetic: 3.72 us -> 0 us
    all_gather x1 -> x0, waiting for transfers between devices: 92.8 us -> none  [body(): lax.all_gather(left_lines, 'east', axis=1, tiled=True)]
    pallas_call x0 -> x1, Pallas kernels: none -> 63.7 us  [body(): pl.pallas_call(kernel, out_shape=jax.ShapeDtypeStruct((ROWS, WIDTH), BF16...]
    all_to_all x2 -> x0, blocking collectives: 36.2 us -> none  [the longest x1 20.2 us: body(): lax.all_to_all(left, 'north', split_axis=2, concat_axis=0, tiled=True)]
    dot_general x7 -> x0, matrix products: 18.1 us -> none  [the longest x1 12.2 us: body(): jnp.einsum('kid,kjd->ijd', lax.all_gather(left_lines, 'east', axis=1, til...]
    all_to_all x1 -> x0, waiting for transfers between devices: 11.2 us -> none  [body(): lax.all_to_all(strip, 'north', split_axis=0, concat_axis=2, tiled=True)]
    convert_element_type x4 -> x0, local copies, waits for them, and re-layouts: 9.56 us -> none  [the longest x1 4.56 us: to_pair(): mixed.astype(jnp.float32)]
    unnamed x24 -> x1, local copies, waits for them, and re-layouts: 11.3 us -> 1.94 us
    all_to_all x1 -> x0, starting transfers between devices: 5.07 us -> none  [body(): lax.all_to_all(strip, 'north', split_axis=0, concat_axis=2, tiled=True)]
  transfers between devices with their start and end apart: 2 -> 0, of which waited for: 2 -> 0; matrix products, arithmetic and copies ran while one was open for 2% -> 0% of each run, Pallas kernels for 0% -> 0%
where the time goes in v2:
time: 66.7 us; the launch traced here: 65.6 us
  Pallas kernels  63.7 us (96%)
  local copies, waits for them, and re-layouts  1.94 us (3%)
    pallas_call x1, Pallas kernels, body(): pl.pallas_call(kernel, out_shape=jax.ShapeDtypeStruct((ROWS, WIDTH), BF16...  63.7 us
    unnamed x1, local copies, waits for them, and re-layouts  1.94 us

profile of v2, /device:TPU:8, one launch (start us, length us, event | category | flops | bytes accessed | tf_op | source)
XLA Modules:
  0.0 65.6 jit_solution(18214228554772741074)
XLA Ops:
  0.0 63.7 %triangle.1 = bf16[2304,128]{1,0:T(8,128)(2,1)} custom-call(bf16[2304,128]{1,0:T(8,128)(2,1)} %bitcast.5, f32[1,128]{1,0:T(1,128)} %bitcast.6, bf16[128,128]{1,0:T(8,128)(2,1)} %lw.1, bf16[128,128]{1,0:T(8,128)(2,1)} %rw.1, bf16[128,128]{1,0:T(8,128)(2,1)} %lg.1, bf16[128,128]{1,0:T(8,128)(2,1)} %rg.1, f32[1,128]{1,0:T(1,128)} %bitcast.7, ...), custom_call_target="tpu_custom_call" | custom-call | tf_op jit(solution)/shard_map/triangle/pallas_call | solution.py:314
  63.7 1.9 %copy.11 = bf16[96,24,128]{2,1,0:T(8,128)(2,1)} copy(bf16[96,24,128]{2,1,0:T(8,128)(2,1)} %bitcast.4) | data formatting | bytes 1179648

commit v3 on v2

v3 whole, which is shorter than its diff:
```python
import jax
import jax.numpy as jnp
from jax import lax
from jax.experimental import pallas as pl
from jax.experimental.pallas import tpu as pltpu
from jax.sharding import PartitionSpec as P

MESH = pl.DeviceIdType.MESH
F32, BF16 = jnp.float32, jnp.bfloat16

RES, WIDTH = 768, 128
NORTH, EAST, PLANE, DEPTH = 8, 32, 16, 8
KB, IB = RES // NORTH, RES // EAST
ROWS = KB * IB
WAVES, WI = 3, 8
LANES = WI * KB
SPAN = 4 * KB
HALF = RES // 2
PIECE = 2 * WI
SIDE = DEPTH * PIECE

STANDS = [y * 48 + c * 24 + w * WI for c in range(2) for w in range(WAVES) for y in range(2)]


def turn(values, amount):
    amount = amount % SPAN
    return values if amount == 0 else pltpu.roll(values, amount, axis=1)


def regroup(parts):
    lane = lax.broadcasted_iota(jnp.int32, parts[0].shape, 1)
    out = []
    for b in range(4):
        row = turn(parts[0], -KB * b)
        for a in range(1, 4):
            row = jnp.where(lane >= KB * a, turn(parts[a], KB * (a - b)), row)
        out.append(row)
    return out


def nt(a, b):
    return lax.dot_general(a, b, (((1,), (1,)), ((), ())), preferred_element_type=F32)


def remote(src, dst, ssem, rsem, where):
    return pltpu.make_async_remote_copy(
        src_ref=src, dst_ref=dst, send_sem=ssem, recv_sem=rsem,
        device_id=where, device_id_type=MESH,
    )


def kernel(
    x_hbm, in_gain_hbm, lw_hbm, rw_hbm, lg_hbm, rg_hbm, mid_gain_hbm, ow_hbm, og_hbm, out_ref,
    x, in_gain, mid_gain, weights, turned, flat, ready, wt, send1, got1, mid, lines, send2, got2,
    left, right, sums, got3, send4, got4, gate, gain_col,
    xs, gs, wsem, s1, r1, s2, r2, sf, rf, s3, r3, s4, r4,
):
    n = lax.axis_index("north")
    e = lax.axis_index("east")
    z, y, c = e // 4, lax.rem(e // 2, 2), lax.rem(e, 2)
    plane = n * 2 + y
    half = z // 4

    def on_plane(p):
        return (p // 2, (z * 2 + lax.rem(p, 2)) * 2 + c)

    def on_line(to_z, to_c):
        return (n, (to_z * 2 + y) * 2 + to_c)

    partner = on_line(z, 1 - c)

    fetch_x = [
        pltpu.make_async_copy(x_hbm.at[:, pl.ds(w * WI, WI), :], x.at[w], xs.at[w])
        for w in range(WAVES)
    ]
    fetch_w = [
        pltpu.make_async_copy(ref, weights.at[p], wsem.at[p])
        for p, ref in enumerate((lw_hbm, lg_hbm, rw_hbm, rg_hbm, ow_hbm, og_hbm))
    ]
    fetch_g = [
        pltpu.make_async_copy(in_gain_hbm, in_gain, gs.at[0]),
        pltpu.make_async_copy(mid_gain_hbm, mid_gain, gs.at[1]),
    ]
    for copy in [fetch_x[0], fetch_g[0], *fetch_w[:2], *fetch_x[1:], *fetch_w[2:], fetch_g[1]]:
        copy.start()

    with jax.named_scope("signal"):
        barrier = pltpu.get_barrier_semaphore()
        for s in range(1, 16):
            t = lax.rem(z * 2 + c + s, 16)
            for where in (on_plane(lax.rem(plane + s, PLANE)), on_line(t // 2, lax.rem(t, 2))):
                pl.semaphore_signal(barrier, inc=1, device_id=where, device_id_type=MESH)

    def normalize(w):
        with jax.named_scope(f"norm#{w}"):
            fetch_x[w].wait()
            if w == 0:
                fetch_g[0].wait()
            v = x[w].astype(F32).reshape(LANES, WIDTH)
            v = v - jnp.mean(v, axis=-1, keepdims=True)
            v = v * lax.rsqrt(jnp.mean(v * v, axis=-1, keepdims=True) + 1e-05) * in_gain[...]
            flat[w * LANES : (w + 1) * LANES, :] = v
            for i in range(WI):
                line = [flat[pl.ds(w * LANES + k * WI + i, WI, stride=WI), :] for k in STANDS]
                at = (w * WI + i) * KB
                ready[at : at + KB, :] = jnp.concatenate(line, axis=0).astype(BF16)

    def orient(a):
        for p in range(2 * a, 2 * a + 2):
            fetch_w[p].wait()
            turned[p] = weights[p].astype(F32).T
            for to in range(DEPTH):
                at = p * WIDTH + to * PLANE
                wt[at : at + PLANE, :] = turned[p, pl.ds(to, PLANE, stride=DEPTH), :].astype(BF16)

    def project(a, w):
        with jax.named_scope(f"project#{a}{w}"):
            for g in range(2):
                rows = ready[w * LANES + g * SPAN : w * LANES + (g + 1) * SPAN, :]
                both = nt(wt[2 * a * WIDTH : 2 * (a + 1) * WIDTH, :], rows)
                both = both[:WIDTH] * jax.nn.sigmoid(both[WIDTH:])
                send1[a, w, :, :, g * SPAN : (g + 1) * SPAN] = both.reshape(DEPTH, PLANE, SPAN).astype(BF16)

    def along(a, w):
        slot, core = (lax.rem(z, 4) * 2 + c, half) if a == 0 else (z, c)
        for s in (1, 7, 2, 6, 3, 5, 4):
            to = lax.rem(z + s, DEPTH)
            remote(
                send1.at[a, w, to], got1.at[a, w, slot], s1.at[a, w], r1.at[a, w], on_line(to, core)
            ).start()
        if a == 1:
            got1[a, w, slot] = send1[a, w, z]
        else:

            @pl.when(c == half)
            def _():
                got1[a, w, slot] = send1[a, w, z]

            @pl.when(c != half)
            def _():
                remote(
                    send1.at[a, w, z], got1.at[a, w, slot], s1.at[a, w], r1.at[a, w], partner
                ).start()

    def pieces(a, w):
        if a == 1:
            yield send1.at[a, w, pl.ds(0, DEPTH - 1)], None
        else:
            yield send1.at[a, w, pl.ds(0, DEPTH - 1)], c == half
            yield send1.at[a, w], c != half

    def across(a, w):
        with jax.named_scope(f"wait1#{a}{w}"):
            for some, when in pieces(a, w):
                take = remote(some, some, s1.at[a, w], r1.at[a, w], partner)
                if when is None:
                    take.wait_recv()
                else:
                    pl.when(when)(take.wait_recv)
        with jax.named_scope(f"across#{a}{w}"):
            for t in range(6):
                for s in range(DEPTH):
                    mid[t, pl.ds(s, PLANE, stride=DEPTH), :] = got1[
                        a, w, s, :, t * 128 : (t + 1) * 128
                    ].astype(F32)
            for d in range(PLANE):
                for t in range(6):
                    send2[a, w, d, :, t * 128 : (t + 1) * 128] = mid[
                        t, d * DEPTH : (d + 1) * DEPTH, :
                    ].astype(BF16)
            for s in range(1, PLANE):
                to = lax.rem(plane + s, PLANE)
                remote(
                    send2.at[a, w, to], got2.at[a, w, plane], s2.at[a, w], r2.at[a, w], on_plane(to)
                ).start()
            got2[a, w, plane] = send2[a, w, plane]

    def settle(a, w):
        with jax.named_scope(f"wait2#{a}{w}"):
            some = send2.at[a, w, pl.ds(0, PLANE - 1)]
            remote(some, some, s2.at[a, w], r2.at[a, w], partner).wait_recv()
        with jax.named_scope(f"settle#{a}{w}"):
            base, step = (w * PIECE, WAVES * PIECE) if a == 0 else (0, PIECE)
            for yy in range(2):
                for g in range(2):
                    for h in range(2):
                        parts = [
                            got2[a, w, (4 * h + q) * 2 + yy, :, g * SPAN : (g + 1) * SPAN].astype(F32)
                            for q in range(4)
                        ]
                        for b, row in enumerate(regroup(parts)):
                            at = pl.ds(base + yy * WI + 4 * g + b, DEPTH, stride=step)
                            for u in range(3):
                                lines[a, 3 * h + u, at, :] = row[:, u * 128 : (u + 1) * 128]
            for t in range(6):
                cols = slice(t * 128, (t + 1) * 128)
                if a == 0:
                    for s in range(DEPTH):
                        rows = slice(s * step + base, s * step + base + PIECE)
                        left[rows, cols] = lines[0, t, rows, :].astype(BF16)
                else:
                    right[w, pl.ds(pl.multiple_of(c * SIDE, SIDE), SIDE), cols] = lines[
                        1, t, :SIDE, :
                    ].astype(BF16)

    orient(0)
    for w in range(WAVES):
        normalize(w)
        project(0, w)
        if w == 0:
            with jax.named_scope("barrier"):
                pl.semaphore_wait(barrier, 30)
        along(0, w)
    orient(1)
    for w in range(WAVES):
        project(1, w)
        along(1, w)

    with jax.named_scope("gate"):
        fetch_w[4].wait()
        fetch_w[5].wait()
        fetch_g[1].wait()
        gain_col[...] = jnp.broadcast_to(mid_gain[...], (WIDTH, WIDTH)).T

        @pl.loop(0, ROWS // SPAN)
        def _(g):
            rows = pl.ds(pl.multiple_of(g * SPAN, SPAN), SPAN)
            gate[rows, :] = jax.nn.sigmoid(
                jnp.dot(ready[rows, :], weights[5], preferred_element_type=F32)
            )

    right_at = pl.ds(pl.multiple_of(c * SIDE + z * PIECE, PIECE), PIECE)

    def share(w):
        mine = right.at[w, pl.ds(pl.multiple_of(c * SIDE, SIDE), SIDE), :]
        return remote(mine, mine, sf.at[w], rf.at[w], partner)

    def multiply(w):
        with jax.named_scope(f"waitshare#{w}"):
            share(w).wait_recv()
        with jax.named_scope(f"mm#{w}"):
            sums[w] = (nt(right[w], left[...]) * RES ** (-0.5)).astype(BF16)
            for s in range(1, 16):
                t = lax.rem(z * 2 + c + s, 16)
                to_z, to_c = t // 2, lax.rem(t, 2)
                at = pl.ds(pl.multiple_of(to_c * SIDE + to_z * PIECE, PIECE), PIECE)
                remote(
                    sums.at[w, at, :],
                    got3.at[w, z, :, pl.ds(pl.multiple_of(c * HALF, HALF), HALF)],
                    s3.at[w], r3.at[w], on_line(to_z, to_c),
                ).start()
            mine = sums[w, right_at, :]

            @pl.when(c == 0)
            def _():
                got3[w, z, :, :HALF] = mine

            @pl.when(c == 1)
            def _():
                got3[w, z, :, HALF:] = mine

    across(0, 0)
    across(0, 1)
    settle(0, 0)
    across(0, 2)
    settle(0, 1)
    across(1, 0)
    settle(0, 2)
    across(1, 1)
    for w in range(WAVES):
        settle(1, w)
        share(w).start()
        multiply(w)
        if w == 0:
            across(1, 2)

    def gather(w):
        with jax.named_scope(f"wait3#{w}"):
            some = sums.at[w, pl.ds(0, 15 * PIECE), :]
            remote(some, some, s3.at[w], r3.at[w], partner).wait_recv()
        with jax.named_scope(f"gather#{w}"):
            for d in range(DEPTH):
                for t in range(6):
                    mid[t, d * PIECE : (d + 1) * PIECE, :] = got3[
                        w, d, :, t * 128 : (t + 1) * 128
                    ].astype(F32)
            for yy in range(2):
                for g in range(2):
                    for h in range(2):
                        parts = [
                            jnp.concatenate(
                                [
                                    mid[3 * h + u, pl.ds(yy * WI + 4 * g + b, DEPTH, stride=PIECE), :]
                                    for u in range(3)
                                ],
                                axis=1,
                            )
                            for b in range(4)
                        ]
                        for q, row in enumerate(regroup(parts)):
                            send4[w, (4 * h + q) * 2 + yy, :, g * SPAN : (g + 1) * SPAN] = row.astype(BF16)
            for s in range(1, PLANE):
                to = lax.rem(plane + s, PLANE)
                remote(send4.at[w, to], got4.at[w, plane], s4.at[w], r4.at[w], on_plane(to)).start()
            got4[w, plane] = send4[w, plane]

    def finish(w):
        with jax.named_scope(f"wait4#{w}"):
            rest = got4.at[w, pl.ds(0, PLANE - 1)]
            remote(rest, rest, s4.at[w], r4.at[w], partner).wait_recv()
        with jax.named_scope(f"finish#{w}"):
            gains = jnp.concatenate([gain_col[...]] * 3, axis=1)
            for g in range(2):
                v = got4[w, :, :, g * SPAN : (g + 1) * SPAN].astype(F32).reshape(WIDTH, SPAN)
                v = v - jnp.mean(v, axis=0, keepdims=True)
                v = v * lax.rsqrt(jnp.mean(v * v, axis=0, keepdims=True) + 1e-05)
                v = (v * gains).astype(BF16)
                out = lax.dot_general(v, weights[4], (((0,), (0,)), ((), ())), preferred_element_type=F32)
                out = out * gate[w * LANES + g * SPAN : w * LANES + (g + 1) * SPAN, :]
                for b in range(4):
                    for p, i in enumerate(STANDS):
                        flat[pl.ds(i * IB + w * WI + 4 * g + b, WI, stride=IB), :] = out[
                            b * KB + p * WI : b * KB + (p + 1) * WI
                        ]

    gather(0)
    gather(1)
    finish(0)
    gather(2)
    finish(1)
    finish(2)

    with jax.named_scope("store"):

        @pl.loop(0, 4)
        def _(b):
            rows = pl.ds(b * (ROWS // 4), ROWS // 4)
            out_ref[rows, :] = flat[rows, :].astype(BF16)

    def sent(ref, sem):
        remote(ref, ref, sem, r4.at[0], partner).wait_send()

    with jax.named_scope("sent"):
        for w in range(WAVES):
            for a in range(2):
                for some, when in pieces(a, w):
                    if when is None:
                        sent(some, s1.at[a, w])
                    else:
                        pl.when(when)(lambda some=some, a=a, w=w: sent(some, s1.at[a, w]))
                sent(send2.at[a, w, pl.ds(0, PLANE - 1)], s2.at[a, w])
            share(w).wait_send()
            sent(sums.at[w, pl.ds(0, 15 * PIECE), :], s3.at[w])
            sent(send4.at[w, pl.ds(0, PLANE - 1)], s4.at[w])


def body(pair_rows, in_gain, left_weight, right_weight, left_gate, right_gate, mid_gain, out_weight, out_gate):
    dma = pltpu.SemaphoreType.DMA
    vmem = pltpu.VMEM
    out = pl.pallas_call(
        kernel,
        out_shape=jax.ShapeDtypeStruct((ROWS, WIDTH), BF16),
        in_specs=[pl.BlockSpec(memory_space=pltpu.MemorySpace.HBM)] * 9,
        out_specs=pl.BlockSpec(memory_space=vmem),
        scratch_shapes=[
            vmem((WAVES, KB, WI, WIDTH), BF16),
            vmem((1, WIDTH), F32),
            vmem((1, WIDTH), F32),
            vmem((6, WIDTH, WIDTH), BF16),
            vmem((4, WIDTH, WIDTH), F32),
            vmem((ROWS, WIDTH), F32),
            vmem((ROWS, WIDTH), BF16),
            vmem((4 * WIDTH, WIDTH), BF16),
            vmem((2, WAVES, DEPTH, PLANE, LANES), BF16),
            vmem((2, WAVES, DEPTH, PLANE, LANES), BF16),
            vmem((6, DEPTH * PLANE, 128), F32),
            vmem((2, 6, HALF, 128), F32),
            vmem((2, WAVES, PLANE, DEPTH, LANES), BF16),
            vmem((2, WAVES, PLANE, DEPTH, LANES), BF16),
            vmem((HALF, RES), BF16),
            vmem((WAVES, 2 * SIDE, RES), BF16),
            vmem((WAVES, 2 * SIDE, HALF), BF16),
            vmem((WAVES, DEPTH, PIECE, RES), BF16),
            vmem((WAVES, PLANE, 8, LANES), BF16),
            vmem((WAVES, PLANE, 8, LANES), BF16),
            vmem((ROWS, WIDTH), F32),
            vmem((WIDTH, WIDTH), F32),
            dma((WAVES,)), dma((2,)), dma((6,)),
            dma((2, WAVES)), dma((2, WAVES)),
            dma((2, WAVES)), dma((2, WAVES)),
            dma((WAVES,)), dma((WAVES,)),
            dma((WAVES,)), dma((WAVES,)),
            dma((WAVES,)), dma((WAVES,)),
        ],
        compiler_params=pltpu.CompilerParams(
            collective_id=0, has_side_effects=True, vmem_limit_bytes=60 * 2**20
        ),
        name="triangle",
    )(
        pair_rows, in_gain.reshape(1, WIDTH), left_weight, right_weight,
        left_gate, right_gate, mid_gain.reshape(1, WIDTH), out_weight, out_gate,
    )
    return out.reshape(KB, IB, WIDTH)


def solution(mesh):
    placed = (P("north", "east", None), P(), P(), P(), P(), P(), P(), P(), P())
    return jax.shard_map(
        body, mesh=mesh, in_specs=placed, out_specs=P("north", "east", None), check_vma=False
    )
```

time: 66.7 us -> 63 us (0.945)
  Pallas kernels: 63.7 us -> 60.3 us
    pallas_call x1, Pallas kernels: 63.7 us -> 60.3 us  [body(): pl.pallas_call(kernel, out_shape=jax.ShapeDtypeStruct((ROWS, WIDTH), BF16...]
where the time goes in v3:
time: 63 us; the launch traced here: 62.2 us
  Pallas kernels  60.3 us (96%)
  local copies, waits for them, and re-layouts  1.94 us (3%)
    pallas_call x1, Pallas kernels, body(): pl.pallas_call(kernel, out_shape=jax.ShapeDtypeStruct((ROWS, WIDTH), BF16...  60.3 us
    unnamed x1, local copies, waits for them, and re-layouts  1.94 us

profile of v3, /device:TPU:8, one launch (start us, length us, event | category | flops | bytes accessed | tf_op | source)
XLA Modules:
  0.0 62.2 jit_solution(9641971261283460247)
XLA Ops:
  0.0 60.3 %triangle.1 = bf16[2304,128]{1,0:T(8,128)(2,1)} custom-call(bf16[96,24,128]{2,1,0:T(8,128)(2,1)} %x_hbm.1, f32[1,128]{1,0:T(1,128)} %bitcast.4, bf16[128,128]{1,0:T(8,128)(2,1)} %lw_hbm.1, bf16[128,128]{1,0:T(8,128)(2,1)} %rw_hbm.1, bf16[128,128]{1,0:T(8,128)(2,1)} %lg_hbm.1, bf16[128,128]{1,0:T(8,128)(2,1)} %rg_hbm.1, f32[1,128]{1,0:T(1,128)} %bitcast.5, ...), custom_call_target="tpu_custom_call" | custom-call | tf_op jit(solution)/shard_map/triangle/pallas_call | solution.py:360
  60.3 1.9 %copy.11 = bf16[96,24,128]{2,1,0:T(8,128)(2,1)} copy(bf16[96,24,128]{2,1,0:T(8,128)(2,1)} %bitcast.3) | data formatting | bytes 1179648

commit v4 on v3

--- a/solution.py
+++ b/solution.py
@@ -15,7 +15,6 @@
 WAVES, WI = 3, 8
 LANES = WI * KB
 SPAN = 4 * KB
-HALF = RES // 2
 PIECE = 2 * WI
 SIDE = DEPTH * PIECE
 
@@ -50,24 +49,23 @@
 
 
 def kernel(
-    x_hbm, in_gain_hbm, lw_hbm, rw_hbm, lg_hbm, rg_hbm, mid_gain_hbm, ow_hbm, og_hbm, out_ref,
+    x_hbm, in_gain_hbm, lw_hbm, rw_hbm, lg_hbm, rg_hbm, mid_gain_hbm, ow_hbm, og_hbm, out_hbm,
     x, in_gain, mid_gain, weights, turned, flat, ready, wt, send1, got1, mid, lines, send2, got2,
-    left, right, sums, got3, send4, got4, gate, gain_col,
-    xs, gs, wsem, s1, r1, s2, r2, sf, rf, s3, r3, s4, r4,
+    left, right, sums, got3, send4, got4, gate, gain_col, done,
+    xs, gs, wsem, s1, r1, s2, r2, sf, rf, s3, r3, s4, r4, ps,
 ):
     n = lax.axis_index("north")
     e = lax.axis_index("east")
     z, y, c = e // 4, lax.rem(e // 2, 2), lax.rem(e, 2)
     plane = n * 2 + y
-    half = z // 4
 
     def on_plane(p):
         return (p // 2, (z * 2 + lax.rem(p, 2)) * 2 + c)
 
-    def on_line(to_z, to_c):
-        return (n, (to_z * 2 + y) * 2 + to_c)
-
-    partner = on_line(z, 1 - c)
+    def on_line(to_z):
+        return (n, (to_z * 2 + y) * 2 + c)
+
+    partner = (n, (z * 2 + y) * 2 + 1 - c)
 
     fetch_x = [
         pltpu.make_async_copy(x_hbm.at[:, pl.ds(w * WI, WI), :], x.at[w], xs.at[w])
@@ -86,10 +84,10 @@
 
     with jax.named_scope("signal"):
         barrier = pltpu.get_barrier_semaphore()
-        for s in range(1, 16):
-            t = lax.rem(z * 2 + c + s, 16)
-            for where in (on_plane(lax.rem(plane + s, PLANE)), on_line(t // 2, lax.rem(t, 2))):
-                pl.semaphore_signal(barrier, inc=1, device_id=where, device_id_type=MESH)
+        partners = [on_plane(lax.rem(plane + s, PLANE)) for s in range(1, PLANE)]
+        partners += [on_line(lax.rem(z + s, DEPTH)) for s in range(1, DEPTH)] + [partner]
+        for where in partners:
+            pl.semaphore_signal(barrier, inc=1, device_id=where, device_id_type=MESH)
 
     def normalize(w):
         with jax.named_scope(f"norm#{w}"):
@@ -122,41 +120,17 @@
                 send1[a, w, :, :, g * SPAN : (g + 1) * SPAN] = both.reshape(DEPTH, PLANE, SPAN).astype(BF16)
 
     def along(a, w):
-        slot, core = (lax.rem(z, 4) * 2 + c, half) if a == 0 else (z, c)
         for s in (1, 7, 2, 6, 3, 5, 4):
             to = lax.rem(z + s, DEPTH)
             remote(
-                send1.at[a, w, to], got1.at[a, w, slot], s1.at[a, w], r1.at[a, w], on_line(to, core)
+                send1.at[a, w, to], got1.at[a, w, z], s1.at[a, w], r1.at[a, w], on_line(to)
             ).start()
-        if a == 1:
-            got1[a, w, slot] = send1[a, w, z]
-        else:
-
-            @pl.when(c == half)
-            def _():
-                got1[a, w, slot] = send1[a, w, z]
-
-            @pl.when(c != half)
-            def _():
-                remote(
-                    send1.at[a, w, z], got1.at[a, w, slot], s1.at[a, w], r1.at[a, w], partner
-                ).start()
-
-    def pieces(a, w):
-        if a == 1:
-            yield send1.at[a, w, pl.ds(0, DEPTH - 1)], None
-        else:
-            yield send1.at[a, w, pl.ds(0, DEPTH - 1)], c == half
-            yield send1.at[a, w], c != half
+        got1[a, w, z] = send1[a, w, z]
 
     def across(a, w):
         with jax.named_scope(f"wait1#{a}{w}"):
-            for some, when in pieces(a, w):
-                take = remote(some, some, s1.at[a, w], r1.at[a, w], partner)
-                if when is None:
-                    take.wait_recv()
-                else:
-                    pl.when(when)(take.wait_recv)
+            some = send1.at[a, w, pl.ds(0, DEPTH - 1)]
+            remote(some, some, s1.at[a, w], r1.at[a, w], partner).wait_recv()
         with jax.named_scope(f"across#{a}{w}"):
             for t in range(6):
                 for s in range(DEPTH):
@@ -174,6 +148,10 @@
                     send2.at[a, w, to], got2.at[a, w, plane], s2.at[a, w], r2.at[a, w], on_plane(to)
                 ).start()
             got2[a, w, plane] = send2[a, w, plane]
+
+    def share(w):
+        mine = left.at[:, c, w]
+        return remote(mine, mine, sf.at[w], rf.at[w], partner)
 
     def settle(a, w):
         with jax.named_scope(f"wait2#{a}{w}"):
@@ -197,11 +175,11 @@
                 if a == 0:
                     for s in range(DEPTH):
                         rows = slice(s * step + base, s * step + base + PIECE)
-                        left[rows, cols] = lines[0, t, rows, :].astype(BF16)
+                        left[s, c, w, :, cols] = lines[0, t, rows, :].astype(BF16)
                 else:
-                    right[w, pl.ds(pl.multiple_of(c * SIDE, SIDE), SIDE), cols] = lines[
-                        1, t, :SIDE, :
-                    ].astype(BF16)
+                    right[w, :, cols] = lines[1, t, :SIDE, :].astype(BF16)
+            if a == 0:
+                share(w).start()
 
     orient(0)
     for w in range(WAVES):
@@ -209,7 +187,7 @@
         project(0, w)
         if w == 0:
             with jax.named_scope("barrier"):
-                pl.semaphore_wait(barrier, 30)
+                pl.semaphore_wait(barrier, PLANE + DEPTH - 1)
         along(0, w)
     orient(1)
     for w in range(WAVES):
@@ -229,35 +207,18 @@
                 jnp.dot(ready[rows, :], weights[5], preferred_element_type=F32)
             )
 
-    right_at = pl.ds(pl.multiple_of(c * SIDE + z * PIECE, PIECE), PIECE)
-
-    def share(w):
-        mine = right.at[w, pl.ds(pl.multiple_of(c * SIDE, SIDE), SIDE), :]
-        return remote(mine, mine, sf.at[w], rf.at[w], partner)
-
     def multiply(w):
-        with jax.named_scope(f"waitshare#{w}"):
-            share(w).wait_recv()
+        if w == 0:
+            with jax.named_scope("waitshare"):
+                for ww in range(WAVES):
+                    share(ww).wait_recv()
         with jax.named_scope(f"mm#{w}"):
-            sums[w] = (nt(right[w], left[...]) * RES ** (-0.5)).astype(BF16)
-            for s in range(1, 16):
-                t = lax.rem(z * 2 + c + s, 16)
-                to_z, to_c = t // 2, lax.rem(t, 2)
-                at = pl.ds(pl.multiple_of(to_c * SIDE + to_z * PIECE, PIECE), PIECE)
-                remote(
-                    sums.at[w, at, :],
-                    got3.at[w, z, :, pl.ds(pl.multiple_of(c * HALF, HALF), HALF)],
-                    s3.at[w], r3.at[w], on_line(to_z, to_c),
-                ).start()
-            mine = sums[w, right_at, :]
-
-            @pl.when(c == 0)
-            def _():
-                got3[w, z, :, :HALF] = mine
-
-            @pl.when(c == 1)
-            def _():
-                got3[w, z, :, HALF:] = mine
+            sums[w] = (nt(right[w], left[...].reshape(RES, RES)) * RES ** (-0.5)).astype(BF16)
+            for s in (1, 7, 2, 6, 3, 5, 4):
+                to = lax.rem(z + s, DEPTH)
+                at = pl.ds(pl.multiple_of(to * PIECE, PIECE), PIECE)
+                remote(sums.at[w, at, :], got3.at[w, z], s3.at[w], r3.at[w], on_line(to)).start()
+            got3[w, z] = sums[w, pl.ds(pl.multiple_of(z * PIECE, PIECE), PIECE), :]
 
     across(0, 0)
     across(0, 1)
@@ -267,16 +228,17 @@
     across(1, 0)
     settle(0, 2)
     across(1, 1)
-    for w in range(WAVES):
-        settle(1, w)
-        share(w).start()
-        multiply(w)
-        if w == 0:
-            across(1, 2)
+    settle(1, 0)
+    multiply(0)
+    across(1, 2)
+    settle(1, 1)
+    multiply(1)
+    settle(1, 2)
+    multiply(2)
 
     def gather(w):
         with jax.named_scope(f"wait3#{w}"):
-            some = sums.at[w, pl.ds(0, 15 * PIECE), :]
+            some = sums.at[w, pl.ds(0, 7 * PIECE), :]
             remote(some, some, s3.at[w], r3.at[w], partner).wait_recv()
         with jax.named_scope(f"gather#{w}"):
             for d in range(DEPTH):
@@ -304,6 +266,11 @@
                 remote(send4.at[w, to], got4.at[w, plane], s4.at[w], r4.at[w], on_plane(to)).start()
             got4[w, plane] = send4[w, plane]
 
+    put = [
+        pltpu.make_async_copy(done.at[w], out_hbm.at[:, pl.ds(w * WI, WI), :], ps.at[w])
+        for w in range(WAVES)
+    ]
+
     def finish(w):
         with jax.named_scope(f"wait4#{w}"):
             rest = got4.at[w, pl.ds(0, PLANE - 1)]
@@ -319,9 +286,11 @@
                 out = out * gate[w * LANES + g * SPAN : w * LANES + (g + 1) * SPAN, :]
                 for b in range(4):
                     for p, i in enumerate(STANDS):
-                        flat[pl.ds(i * IB + w * WI + 4 * g + b, WI, stride=IB), :] = out[
+                        flat[pl.ds(w * LANES + i * WI + 4 * g + b, WI, stride=WI), :] = out[
                             b * KB + p * WI : b * KB + (p + 1) * WI
                         ]
+            done[w] = flat[w * LANES : (w + 1) * LANES, :].reshape(KB, WI, WIDTH).astype(BF16)
+            put[w].start()
 
     gather(0)
     gather(1)
@@ -330,38 +299,28 @@
     finish(1)
     finish(2)
 
-    with jax.named_scope("store"):
-
-        @pl.loop(0, 4)
-        def _(b):
-            rows = pl.ds(b * (ROWS // 4), ROWS // 4)
-            out_ref[rows, :] = flat[rows, :].astype(BF16)
-
     def sent(ref, sem):
         remote(ref, ref, sem, r4.at[0], partner).wait_send()
 
     with jax.named_scope("sent"):
         for w in range(WAVES):
+            put[w].wait()
             for a in range(2):
-                for some, when in pieces(a, w):
-                    if when is None:
-                        sent(some, s1.at[a, w])
-                    else:
-                        pl.when(when)(lambda some=some, a=a, w=w: sent(some, s1.at[a, w]))
+                sent(send1.at[a, w, pl.ds(0, DEPTH - 1)], s1.at[a, w])
                 sent(send2.at[a, w, pl.ds(0, PLANE - 1)], s2.at[a, w])
             share(w).wait_send()
-            sent(sums.at[w, pl.ds(0, 15 * PIECE), :], s3.at[w])
+            sent(sums.at[w, pl.ds(0, 7 * PIECE), :], s3.at[w])
             sent(send4.at[w, pl.ds(0, PLANE - 1)], s4.at[w])
 
 
 def body(pair_rows, in_gain, left_weight, right_weight, left_gate, right_gate, mid_gain, out_weight, out_gate):
     dma = pltpu.SemaphoreType.DMA
     vmem = pltpu.VMEM
-    out = pl.pallas_call(
+    return pl.pallas_call(
         kernel,
-        out_shape=jax.ShapeDtypeStruct((ROWS, WIDTH), BF16),
+        out_shape=jax.ShapeDtypeStruct((KB, IB, WIDTH), BF16),
         in_specs=[pl.BlockSpec(memory_space=pltpu.MemorySpace.HBM)] * 9,
-        out_specs=pl.BlockSpec(memory_space=vmem),
+        out_specs=pl.BlockSpec(memory_space=pltpu.MemorySpace.HBM),
         scratch_shapes=[
             vmem((WAVES, KB, WI, WIDTH), BF16),
             vmem((1, WIDTH), F32),
@@ -374,23 +333,25 @@
             vmem((2, WAVES, DEPTH, PLANE, LANES), BF16),
             vmem((2, WAVES, DEPTH, PLANE, LANES), BF16),
             vmem((6, DEPTH * PLANE, 128), F32),
-            vmem((2, 6, HALF, 128), F32),
+            vmem((2, 6, RES // 2, 128), F32),
             vmem((2, WAVES, PLANE, DEPTH, LANES), BF16),
             vmem((2, WAVES, PLANE, DEPTH, LANES), BF16),
-            vmem((HALF, RES), BF16),
-            vmem((WAVES, 2 * SIDE, RES), BF16),
-            vmem((WAVES, 2 * SIDE, HALF), BF16),
+            vmem((DEPTH, 2, WAVES, PIECE, RES), BF16),
+            vmem((WAVES, SIDE, RES), BF16),
+            vmem((WAVES, SIDE, RES), BF16),
             vmem((WAVES, DEPTH, PIECE, RES), BF16),
             vmem((WAVES, PLANE, 8, LANES), BF16),
             vmem((WAVES, PLANE, 8, LANES), BF16),
             vmem((ROWS, WIDTH), F32),
             vmem((WIDTH, WIDTH), F32),
+            vmem((WAVES, KB, WI, WIDTH), BF16),
             dma((WAVES,)), dma((2,)), dma((6,)),
             dma((2, WAVES)), dma((2, WAVES)),
             dma((2, WAVES)), dma((2, WAVES)),
             dma((WAVES,)), dma((WAVES,)),
             dma((WAVES,)), dma((WAVES,)),
             dma((WAVES,)), dma((WAVES,)),
+            dma((WAVES,)),
         ],
         compiler_params=pltpu.CompilerParams(
             collective_id=0, has_side_effects=True, vmem_limit_bytes=60 * 2**20
@@ -400,7 +361,6 @@
         pair_rows, in_gain.reshape(1, WIDTH), left_weight, right_weight,
         left_gate, right_gate, mid_gain.reshape(1, WIDTH), out_weight, out_gate,
     )
-    return out.reshape(KB, IB, WIDTH)
 
 
 def solution(mesh):

time: 63 us -> 60.6 us (0.962)
  Pallas kernels: 60.3 us -> 58.5 us
    pallas_call x1, Pallas kernels: 60.3 us -> 58.5 us  [body(): pl.pallas_call(kernel, out_shape=jax.ShapeDtypeStruct((KB, IB, WIDTH), BF...]
where the time goes in v4:
time: 60.6 us; the launch traced here: 60.4 us
  Pallas kernels  58.5 us (97%)
  local copies, waits for them, and re-layouts  1.94 us (3%)
    pallas_call x1, Pallas kernels, body(): pl.pallas_call(kernel, out_shape=jax.ShapeDtypeStruct((KB, IB, WIDTH), BF...  58.5 us
    unnamed x1, local copies, waits for them, and re-layouts  1.94 us

profile of v4, /device:TPU:8, one launch (start us, length us, event | category | flops | bytes accessed | tf_op | source)
XLA Modules:
  0.0 60.4 jit_solution(3496822695504954185)
XLA Ops:
  0.0 58.5 %triangle.1 = bf16[96,24,128]{2,1,0:T(8,128)(2,1)} custom-call(bf16[96,24,128]{2,1,0:T(8,128)(2,1)} %x_hbm.1, f32[1,128]{1,0:T(1,128)} %bitcast.2, bf16[128,128]{1,0:T(8,128)(2,1)} %lw_hbm.1, bf16[128,128]{1,0:T(8,128)(2,1)} %rw_hbm.1, bf16[128,128]{1,0:T(8,128)(2,1)} %lg_hbm.1, bf16[128,128]{1,0:T(8,128)(2,1)} %rg_hbm.1, f32[1,128]{1,0:T(1,128)} %bitcast.3, ...), custom_call_target="tpu_custom_call" | custom-call | tf_op jit(solution)/shard_map/triangle/pallas_call | solution.py:319
  58.5 1.9 %copy.11 = bf16[96,24,128]{2,1,0:T(8,128)(2,1)} copy(bf16[96,24,128]{2,1,0:T(8,128)(2,1)} %triangle.1) | data formatting | bytes 1179648

commit v5 on v4

--- a/solution.py
+++ b/solution.py
@@ -19,6 +19,13 @@
 SIDE = DEPTH * PIECE
 
 STANDS = [y * 48 + c * 24 + w * WI for c in range(2) for w in range(WAVES) for y in range(2)]
+
+
+ACROSS = sorted(
+    ((dx, dy) for dx in range(4) for dy in range(4) if dx or dy),
+    key=lambda step: -sum(min(d, 4 - d) for d in step),
+)
+ALONG = (4, 3, 5, 2, 6, 1, 7)
 
 
 def turn(values, amount):
@@ -59,8 +66,12 @@
     z, y, c = e // 4, lax.rem(e // 2, 2), lax.rem(e, 2)
     plane = n * 2 + y
 
-    def on_plane(p):
-        return (p // 2, (z * 2 + lax.rem(p, 2)) * 2 + c)
+    px, py = lax.rem(n, 4), (n // 4) * 2 + y
+
+    def on_plane(step):
+        x_to, y_to = lax.rem(px + step[0], 4), lax.rem(py + step[1], 4)
+        n_to, y_to = (y_to // 2) * 4 + x_to, lax.rem(y_to, 2)
+        return n_to * 2 + y_to, (n_to, (z * 2 + y_to) * 2 + c)
 
     def on_line(to_z):
         return (n, (to_z * 2 + y) * 2 + c)
@@ -84,7 +95,7 @@
 
     with jax.named_scope("signal"):
         barrier = pltpu.get_barrier_semaphore()
-        partners = [on_plane(lax.rem(plane + s, PLANE)) for s in range(1, PLANE)]
+        partners = [on_plane(step)[1] for step in ACROSS]
         partners += [on_line(lax.rem(z + s, DEPTH)) for s in range(1, DEPTH)] + [partner]
         for where in partners:
             pl.semaphore_signal(barrier, inc=1, device_id=where, device_id_type=MESH)
@@ -120,7 +131,7 @@
                 send1[a, w, :, :, g * SPAN : (g + 1) * SPAN] = both.reshape(DEPTH, PLANE, SPAN).astype(BF16)
 
     def along(a, w):
-        for s in (1, 7, 2, 6, 3, 5, 4):
+        for s in ALONG:
             to = lax.rem(z + s, DEPTH)
             remote(
                 send1.at[a, w, to], got1.at[a, w, z], s1.at[a, w], r1.at[a, w], on_line(to)
@@ -142,10 +153,10 @@
                     send2[a, w, d, :, t * 128 : (t + 1) * 128] = mid[
                         t, d * DEPTH : (d + 1) * DEPTH, :
                     ].astype(BF16)
-            for s in range(1, PLANE):
-                to = lax.rem(plane + s, PLANE)
+            for step in ACROSS:
+                to, where = on_plane(step)
                 remote(
-                    send2.at[a, w, to], got2.at[a, w, plane], s2.at[a, w], r2.at[a, w], on_plane(to)
+                    send2.at[a, w, to], got2.at[a, w, plane], s2.at[a, w], r2.at[a, w], where
                 ).start()
             got2[a, w, plane] = send2[a, w, plane]
 
@@ -214,7 +225,7 @@
                     share(ww).wait_recv()
         with jax.named_scope(f"mm#{w}"):
             sums[w] = (nt(right[w], left[...].reshape(RES, RES)) * RES ** (-0.5)).astype(BF16)
-            for s in (1, 7, 2, 6, 3, 5, 4):
+            for s in ALONG:
                 to = lax.rem(z + s, DEPTH)
                 at = pl.ds(pl.multiple_of(to * PIECE, PIECE), PIECE)
                 remote(sums.at[w, at, :], got3.at[w, z], s3.at[w], r3.at[w], on_line(to)).start()
@@ -261,9 +272,9 @@
                         ]
                         for q, row in enumerate(regroup(parts)):
                             send4[w, (4 * h + q) * 2 + yy, :, g * SPAN : (g + 1) * SPAN] = row.astype(BF16)
-            for s in range(1, PLANE):
-                to = lax.rem(plane + s, PLANE)
-                remote(send4.at[w, to], got4.at[w, plane], s4.at[w], r4.at[w], on_plane(to)).start()
+            for step in ACROSS:
+                to, where = on_plane(step)
+                remote(send4.at[w, to], got4.at[w, plane], s4.at[w], r4.at[w], where).start()
             got4[w, plane] = send4[w, plane]
 
     put = [

time: 60.6 us -> 58.1 us (0.959)
  Pallas kernels: 58.5 us -> 55.8 us
    pallas_call x1, Pallas kernels: 58.5 us -> 55.8 us  [body(): pl.pallas_call(kernel, out_shape=jax.ShapeDtypeStruct((KB, IB, WIDTH), BF...]
where the time goes in v5:
time: 58.1 us; the launch traced here: 57.7 us
  Pallas kernels  55.8 us (96%)
  local copies, waits for them, and re-layouts  1.94 us (3%)
    pallas_call x1, Pallas kernels, body(): pl.pallas_call(kernel, out_shape=jax.ShapeDtypeStruct((KB, IB, WIDTH), BF...  55.8 us
    unnamed x1, local copies, waits for them, and re-layouts  1.94 us

profile of v5, /device:TPU:8, one launch (start us, length us, event | category | flops | bytes accessed | tf_op | source)
XLA Modules:
  0.0 57.7 jit_solution(255943474519347313)
XLA Ops:
  0.0 55.8 %triangle.1 = bf16[96,24,128]{2,1,0:T(8,128)(2,1)} custom-call(bf16[96,24,128]{2,1,0:T(8,128)(2,1)} %x_hbm.1, f32[1,128]{1,0:T(1,128)} %bitcast.2, bf16[128,128]{1,0:T(8,128)(2,1)} %lw_hbm.1, bf16[128,128]{1,0:T(8,128)(2,1)} %rw_hbm.1, bf16[128,128]{1,0:T(8,128)(2,1)} %lg_hbm.1, bf16[128,128]{1,0:T(8,128)(2,1)} %rg_hbm.1, f32[1,128]{1,0:T(1,128)} %bitcast.3, ...), custom_call_target="tpu_custom_call" | custom-call | tf_op jit(solution)/shard_map/triangle/pallas_call | solution.py:330
  55.8 1.9 %copy.11 = bf16[96,24,128]{2,1,0:T(8,128)(2,1)} copy(bf16[96,24,128]{2,1,0:T(8,128)(2,1)} %triangle.1) | data formatting | bytes 1179648

commit v6 on v5

--- a/solution.py
+++ b/solution.py
@@ -58,8 +58,8 @@
 def kernel(
     x_hbm, in_gain_hbm, lw_hbm, rw_hbm, lg_hbm, rg_hbm, mid_gain_hbm, ow_hbm, og_hbm, out_hbm,
     x, in_gain, mid_gain, weights, turned, flat, ready, wt, send1, got1, mid, lines, send2, got2,
-    left, right, sums, got3, send4, got4, gate, gain_col, done,
-    xs, gs, wsem, s1, r1, s2, r2, sf, rf, s3, r3, s4, r4, ps,
+    left, right, sums, got3, send4, got4, gate, gain_col,
+    xs, gs, wsem, s1, r1, s2, r2, sf, rf, s3, r3, s4, r4,
 ):
     n = lax.axis_index("north")
     e = lax.axis_index("east")
@@ -277,11 +277,6 @@
                 remote(send4.at[w, to], got4.at[w, plane], s4.at[w], r4.at[w], where).start()
             got4[w, plane] = send4[w, plane]
 
-    put = [
-        pltpu.make_async_copy(done.at[w], out_hbm.at[:, pl.ds(w * WI, WI), :], ps.at[w])
-        for w in range(WAVES)
-    ]
-
     def finish(w):
         with jax.named_scope(f"wait4#{w}"):
             rest = got4.at[w, pl.ds(0, PLANE - 1)]
@@ -300,8 +295,7 @@
                         flat[pl.ds(w * LANES + i * WI + 4 * g + b, WI, stride=WI), :] = out[
                             b * KB + p * WI : b * KB + (p + 1) * WI
                         ]
-            done[w] = flat[w * LANES : (w + 1) * LANES, :].reshape(KB, WI, WIDTH).astype(BF16)
-            put[w].start()
+            out_hbm[:, w * WI : (w + 1) * WI, :] = flat[w * LANES : (w + 1) * LANES, :].reshape(KB, WI, WIDTH).astype(BF16)
 
     gather(0)
     gather(1)
@@ -315,7 +309,6 @@
 
     with jax.named_scope("sent"):
         for w in range(WAVES):
-            put[w].wait()
             for a in range(2):
                 sent(send1.at[a, w, pl.ds(0, DEPTH - 1)], s1.at[a, w])
                 sent(send2.at[a, w, pl.ds(0, PLANE - 1)], s2.at[a, w])
@@ -329,9 +322,9 @@
     vmem = pltpu.VMEM
     return pl.pallas_call(
         kernel,
-        out_shape=jax.ShapeDtypeStruct((KB, IB, WIDTH), BF16),
+        out_shape=pltpu.VMEM((KB, IB, WIDTH), BF16),
         in_specs=[pl.BlockSpec(memory_space=pltpu.MemorySpace.HBM)] * 9,
-        out_specs=pl.BlockSpec(memory_space=pltpu.MemorySpace.HBM),
+        out_specs=pl.BlockSpec(memory_space=vmem),
         scratch_shapes=[
             vmem((WAVES, KB, WI, WIDTH), BF16),
             vmem((1, WIDTH), F32),
@@ -355,22 +348,25 @@
             vmem((WAVES, PLANE, 8, LANES), BF16),
             vmem((ROWS, WIDTH), F32),
             vmem((WIDTH, WIDTH), F32),
-            vmem((WAVES, KB, WI, WIDTH), BF16),
             dma((WAVES,)), dma((2,)), dma((6,)),
             dma((2, WAVES)), dma((2, WAVES)),
             dma((2, WAVES)), dma((2, WAVES)),
             dma((WAVES,)), dma((WAVES,)),
             dma((WAVES,)), dma((WAVES,)),
             dma((WAVES,)), dma((WAVES,)),
-            dma((WAVES,)),
         ],
         compiler_params=pltpu.CompilerParams(
             collective_id=0, has_side_effects=True, vmem_limit_bytes=60 * 2**20
         ),
         name="triangle",
     )(
-        pair_rows, in_gain.reshape(1, WIDTH), left_weight, right_weight,
-        left_gate, right_gate, mid_gain.reshape(1, WIDTH), out_weight, out_gate,
+        *(
+            pltpu.with_memory_space_constraint(v, pltpu.MemorySpace.HBM)
+            for v in (
+                pair_rows, in_gain.reshape(1, WIDTH), left_weight, right_weight,
+                left_gate, right_gate, mid_gain.reshape(1, WIDTH), out_weight, out_gate,
+            )
+        )
     )
 
 

time: 58.1 us -> 56.2 us (0.967)
  local copies, waits for them, and re-layouts: 1.94 us -> 0.82 us
  Pallas kernels: 55.8 us -> 55.1 us
    unnamed x1, local copies, waits for them, and re-layouts: 1.94 us -> 0.82 us
    pallas_call x1, Pallas kernels: 55.8 us -> 55.1 us  [body(): pl.pallas_call(kernel, out_shape=pltpu.VMEM((KB, IB, WIDTH), BF16), in_sp...]
where the time goes in v6:
time: 56.2 us; the launch traced here: 55.9 us
  Pallas kernels  55.1 us (98%)
  local copies, waits for them, and re-layouts  0.82 us (1%)
    pallas_call x1, Pallas kernels, body(): pl.pallas_call(kernel, out_shape=pltpu.VMEM((KB, IB, WIDTH), BF16), in_sp...  55.1 us

profile of v6, /device:TPU:8, one launch (start us, length us, event | category | flops | bytes accessed | tf_op | source)
XLA Modules:
  0.0 55.9 jit_solution(9885585436683092782)
XLA Ops:
  0.0 55.1 %triangle.1 = bf16[96,24,128]{2,1,0:T(8,128)(2,1)S(1)} custom-call(bf16[96,24,128]{2,1,0:T(8,128)(2,1)} %x_hbm.1, f32[1,128]{1,0:T(1,128)} %bitcast.2, bf16[128,128]{1,0:T(8,128)(2,1)} %lw_hbm.1, bf16[128,128]{1,0:T(8,128)(2,1)} %rw_hbm.1, bf16[128,128]{1,0:T(8,128)(2,1)} %lg_hbm.1, bf16[128,128]{1,0:T(8,128)(2,1)} %rg_hbm.1, f32[1,128]{1,0:T(1,128)} %bitcast.3, ...), custom_call_target="tpu_custom_call" | custom-call | tf_op jit(solution)/shard_map/triangle/pallas_call | solution.py:323
  55.1 0.8 %copy.11 = bf16[96,24,128]{2,1,0:T(8,128)(2,1)} copy(bf16[96,24,128]{2,1,0:T(8,128)(2,1)S(1)} %triangle.1) | data formatting | bytes 1179648

commit v7 on v6

--- a/solution.py
+++ b/solution.py
@@ -25,7 +25,7 @@
     ((dx, dy) for dx in range(4) for dy in range(4) if dx or dy),
     key=lambda step: -sum(min(d, 4 - d) for d in step),
 )
-ALONG = (4, 3, 5, 2, 6, 1, 7)
+ALONG = (3, 2, 1)
 
 
 def turn(values, amount):
@@ -59,7 +59,7 @@
     x_hbm, in_gain_hbm, lw_hbm, rw_hbm, lg_hbm, rg_hbm, mid_gain_hbm, ow_hbm, og_hbm, out_hbm,
     x, in_gain, mid_gain, weights, turned, flat, ready, wt, send1, got1, mid, lines, send2, got2,
     left, right, sums, got3, send4, got4, gate, gain_col,
-    xs, gs, wsem, s1, r1, s2, r2, sf, rf, s3, r3, s4, r4,
+    xs, gs, wsem, s1, r1, s2, r2, sf, rf, sn, rn, sq, rq, s3, r3, s4, r4,
 ):
     n = lax.axis_index("north")
     e = lax.axis_index("east")
@@ -72,6 +72,9 @@
         x_to, y_to = lax.rem(px + step[0], 4), lax.rem(py + step[1], 4)
         n_to, y_to = (y_to // 2) * 4 + x_to, lax.rem(y_to, 2)
         return n_to * 2 + y_to, (n_to, (z * 2 + y_to) * 2 + c)
+
+    def off(s):
+        return lax.rem(z + (s + DEPTH), DEPTH)
 
     def on_line(to_z):
         return (n, (to_z * 2 + y) * 2 + c)
@@ -96,7 +99,7 @@
     with jax.named_scope("signal"):
         barrier = pltpu.get_barrier_semaphore()
         partners = [on_plane(step)[1] for step in ACROSS]
-        partners += [on_line(lax.rem(z + s, DEPTH)) for s in range(1, DEPTH)] + [partner]
+        partners += [on_line(off(s)) for s in (1, 2, 3, -1, -2, -3)] + [partner]
         for where in partners:
             pl.semaphore_signal(barrier, inc=1, device_id=where, device_id_type=MESH)
 
@@ -132,15 +135,16 @@
 
     def along(a, w):
         for s in ALONG:
-            to = lax.rem(z + s, DEPTH)
-            remote(
-                send1.at[a, w, to], got1.at[a, w, z], s1.at[a, w], r1.at[a, w], on_line(to)
-            ).start()
-        got1[a, w, z] = send1[a, w, z]
+            for group, slot, to in ((off(s), s, off(s)), (off(-1 - s), 4 + s, off(-s))):
+                remote(
+                    send1.at[a, w, group], got1.at[a, w, slot], s1.at[a, w], r1.at[a, w], on_line(to)
+                ).start()
+        got1[a, w, 0] = send1[a, w, z]
+        got1[a, w, 4] = send1[a, w, off(-1)]
 
     def across(a, w):
         with jax.named_scope(f"wait1#{a}{w}"):
-            some = send1.at[a, w, pl.ds(0, DEPTH - 1)]
+            some = send1.at[a, w, pl.ds(0, 6)]
             remote(some, some, s1.at[a, w], r1.at[a, w], partner).wait_recv()
         with jax.named_scope(f"across#{a}{w}"):
             for t in range(6):
@@ -160,9 +164,24 @@
                 ).start()
             got2[a, w, plane] = send2[a, w, plane]
 
+    here = [(0, off(-s)) for s in range(4)] + [(1, off(s)) for s in range(4)]
+    there = [(1, off(-1 - s)) for s in range(4)] + [(0, off(1 + s)) for s in range(4)]
+
     def share(w):
-        mine = left.at[:, c, w]
-        return remote(mine, mine, sf.at[w], rf.at[w], partner)
+        for ch, line in here:
+            mine = left.at[ch, line, c, w]
+            to = on_line(off(1) if ch == 0 else off(-1))
+            remote(mine, left.at[1 - ch, line, c, w], sn.at[w], rn.at[w], to).start()
+        for ch, line in here:
+            mine = left.at[ch, line, c, w]
+            remote(mine, mine, sf.at[w], rf.at[w], partner).start()
+
+    def hand_on(w):
+        with jax.named_scope(f"hand#{w}"):
+            remote(send1.at[0, w], send1.at[0, w], sn.at[w], rn.at[w], partner).wait_recv()
+            for ch, line in there:
+                mine = left.at[ch, line, c, w]
+                remote(mine, mine, sq.at[w], rq.at[w], partner).start()
 
     def settle(a, w):
         with jax.named_scope(f"wait2#{a}{w}"):
@@ -186,11 +205,11 @@
                 if a == 0:
                     for s in range(DEPTH):
                         rows = slice(s * step + base, s * step + base + PIECE)
-                        left[s, c, w, :, cols] = lines[0, t, rows, :].astype(BF16)
+                        left[*here[s], c, w, :, cols] = lines[0, t, rows, :].astype(BF16)
                 else:
                     right[w, :, cols] = lines[1, t, :SIDE, :].astype(BF16)
             if a == 0:
-                share(w).start()
+                share(w)
 
     orient(0)
     for w in range(WAVES):
@@ -198,12 +217,13 @@
         project(0, w)
         if w == 0:
             with jax.named_scope("barrier"):
-                pl.semaphore_wait(barrier, PLANE + DEPTH - 1)
+                pl.semaphore_wait(barrier, PLANE + 6)
         along(0, w)
     orient(1)
     for w in range(WAVES):
         project(1, w)
-        along(1, w)
+        if w < 2:
+            along(1, w)
 
     with jax.named_scope("gate"):
         fetch_w[4].wait()
@@ -222,14 +242,20 @@
         if w == 0:
             with jax.named_scope("waitshare"):
                 for ww in range(WAVES):
-                    share(ww).wait_recv()
+                    for ssem, rsem in ((sf, rf), (sq, rq)):
+                        remote(send1.at[0, ww], send1.at[0, ww], ssem.at[ww], rsem.at[ww], partner).wait_recv()
         with jax.named_scope(f"mm#{w}"):
-            sums[w] = (nt(right[w], left[...].reshape(RES, RES)) * RES ** (-0.5)).astype(BF16)
-            for s in ALONG:
-                to = lax.rem(z + s, DEPTH)
-                at = pl.ds(pl.multiple_of(to * PIECE, PIECE), PIECE)
-                remote(sums.at[w, at, :], got3.at[w, z], s3.at[w], r3.at[w], on_line(to)).start()
-            got3[w, z] = sums[w, pl.ds(pl.multiple_of(z * PIECE, PIECE), PIECE), :]
+            for ch in range(2):
+                rows = slice(ch * SIDE // 2, (ch + 1) * SIDE // 2)
+                sums[w, rows, :] = (nt(right[w, rows, :], left[ch].reshape(RES, RES)) * RES ** (-0.5)).astype(BF16)
+                group = off(-ch)
+                for s in ALONG:
+                    at = ch * SIDE // 2 + s * PIECE
+                    remote(
+                        sums.at[w, pl.ds(at, PIECE), :], got3.at[w, group], s3.at[w], r3.at[w],
+                        on_line(off(-s if ch == 0 else s)),
+                    ).start()
+                got3[w, group] = sums[w, ch * SIDE // 2 : ch * SIDE // 2 + PIECE, :]
 
     across(0, 0)
     across(0, 1)
@@ -238,18 +264,22 @@
     settle(0, 1)
     across(1, 0)
     settle(0, 2)
+    along(1, 2)
     across(1, 1)
+    hand_on(0)
     settle(1, 0)
+    hand_on(1)
+    settle(1, 1)
+    hand_on(2)
+    across(1, 2)
     multiply(0)
-    across(1, 2)
-    settle(1, 1)
     multiply(1)
     settle(1, 2)
     multiply(2)
 
     def gather(w):
         with jax.named_scope(f"wait3#{w}"):
-            some = sums.at[w, pl.ds(0, 7 * PIECE), :]
+            some = sums.at[w, pl.ds(0, 6 * PIECE), :]
             remote(some, some, s3.at[w], r3.at[w], partner).wait_recv()
         with jax.named_scope(f"gather#{w}"):
             for d in range(DEPTH):
@@ -299,8 +329,8 @@
 
     gather(0)
     gather(1)
+    gather(2)
     finish(0)
-    gather(2)
     finish(1)
     finish(2)
 
@@ -310,10 +340,11 @@
     with jax.named_scope("sent"):
         for w in range(WAVES):
             for a in range(2):
-                sent(send1.at[a, w, pl.ds(0, DEPTH - 1)], s1.at[a, w])
+                sent(send1.at[a, w, pl.ds(0, 6)], s1.at[a, w])
                 sent(send2.at[a, w, pl.ds(0, PLANE - 1)], s2.at[a, w])
-            share(w).wait_send()
-            sent(sums.at[w, pl.ds(0, 7 * PIECE), :], s3.at[w])
+            for sem in (sf, sn, sq):
+                sent(send1.at[0, w], sem.at[w])
+            sent(sums.at[w, pl.ds(0, 6 * PIECE), :], s3.at[w])
             sent(send4.at[w, pl.ds(0, PLANE - 1)], s4.at[w])
 
 
@@ -340,7 +371,7 @@
             vmem((2, 6, RES // 2, 128), F32),
             vmem((2, WAVES, PLANE, DEPTH, LANES), BF16),
             vmem((2, WAVES, PLANE, DEPTH, LANES), BF16),
-            vmem((DEPTH, 2, WAVES, PIECE, RES), BF16),
+            vmem((2, DEPTH, 2, WAVES, PIECE, RES), BF16),
             vmem((WAVES, SIDE, RES), BF16),
             vmem((WAVES, SIDE, RES), BF16),
             vmem((WAVES, DEPTH, PIECE, RES), BF16),
@@ -351,6 +382,8 @@
             dma((WAVES,)), dma((2,)), dma((6,)),
             dma((2, WAVES)), dma((2, WAVES)),
             dma((2, WAVES)), dma((2, WAVES)),
+            dma((WAVES,)), dma((WAVES,)),
+            dma((WAVES,)), dma((WAVES,)),
             dma((WAVES,)), dma((WAVES,)),
             dma((WAVES,)), dma((WAVES,)),
             dma((WAVES,)), dma((WAVES,)),

time: 56.2 us -> 55.9 us (level); the launches traced: 55.9 us -> 55 us
  Pallas kernels: 55.1 us -> 54.2 us
    pallas_call x1, Pallas kernels: 55.1 us -> 54.2 us  [body(): pl.pallas_call(kernel, out_shape=pltpu.VMEM((KB, IB, WIDTH), BF16), in_sp...]
where the time goes in v7:
time: 55.9 us; the launch traced here: 55 us
  Pallas kernels  54.2 us (97%)
  local copies, waits for them, and re-layouts  0.82 us (1%)
    pallas_call x1, Pallas kernels, body(): pl.pallas_call(kernel, out_shape=pltpu.VMEM((KB, IB, WIDTH), BF16), in_sp...  54.2 us

profile of v7, /device:TPU:8, one launch (start us, length us, event | category | flops | bytes accessed | tf_op | source)
XLA Modules:
  0.0 55.0 jit_solution(7479203212108211058)
XLA Ops:
  0.0 54.2 %triangle.1 = bf16[96,24,128]{2,1,0:T(8,128)(2,1)S(1)} custom-call(bf16[96,24,128]{2,1,0:T(8,128)(2,1)} %x_hbm.1, f32[1,128]{1,0:T(1,128)} %bitcast.2, bf16[128,128]{1,0:T(8,128)(2,1)} %lw_hbm.1, bf16[128,128]{1,0:T(8,128)(2,1)} %rw_hbm.1, bf16[128,128]{1,0:T(8,128)(2,1)} %lg_hbm.1, bf16[128,128]{1,0:T(8,128)(2,1)} %rg_hbm.1, f32[1,128]{1,0:T(1,128)} %bitcast.3, ...), custom_call_target="tpu_custom_call" | custom-call | tf_op jit(solution)/shard_map/triangle/pallas_call | solution.py:354
  54.2 0.8 %copy.11 = bf16[96,24,128]{2,1,0:T(8,128)(2,1)} copy(bf16[96,24,128]{2,1,0:T(8,128)(2,1)S(1)} %triangle.1) | data formatting | bytes 1179648

commit v8 on v7

--- a/solution.py
+++ b/solution.py
@@ -168,7 +168,8 @@
     there = [(1, off(-1 - s)) for s in range(4)] + [(0, off(1 + s)) for s in range(4)]
 
     def share(w):
-        for ch, line in here:
+        for s in (0, 4, 1, 5, 2, 6, 3, 7):
+            ch, line = here[s]
             mine = left.at[ch, line, c, w]
             to = on_line(off(1) if ch == 0 else off(-1))
             remote(mine, left.at[1 - ch, line, c, w], sn.at[w], rn.at[w], to).start()

time: 55.9 us -> 55.9 us (level)
  no operation moved by 1% of the time
where the time goes in v8:
time: 55.9 us; the launch traced here: 55 us
  Pallas kernels  54.1 us (97%)
  local copies, waits for them, and re-layouts  0.82 us (1%)
    pallas_call x1, Pallas kernels, body(): pl.pallas_call(kernel, out_shape=pltpu.VMEM((KB, IB, WIDTH), BF16), in_sp...  54.1 us

profile of v8, /device:TPU:8, one launch (start us, length us, event | category | flops | bytes accessed | tf_op | source)
XLA Modules:
  0.0 55.0 jit_solution(15937084428006708429)
XLA Ops:
  0.0 54.1 %triangle.1 = bf16[96,24,128]{2,1,0:T(8,128)(2,1)S(1)} custom-call(bf16[96,24,128]{2,1,0:T(8,128)(2,1)} %x_hbm.1, f32[1,128]{1,0:T(1,128)} %bitcast.2, bf16[128,128]{1,0:T(8,128)(2,1)} %lw_hbm.1, bf16[128,128]{1,0:T(8,128)(2,1)} %rw_hbm.1, bf16[128,128]{1,0:T(8,128)(2,1)} %lg_hbm.1, bf16[128,128]{1,0:T(8,128)(2,1)} %rg_hbm.1, f32[1,128]{1,0:T(1,128)} %bitcast.3, ...), custom_call_target="tpu_custom_call" | custom-call | tf_op jit(solution)/shard_map/triangle/pallas_call | solution.py:355
  54.2 0.8 %copy.11 = bf16[96,24,128]{2,1,0:T(8,128)(2,1)} copy(bf16[96,24,128]{2,1,0:T(8,128)(2,1)S(1)} %triangle.1) | data formatting | bytes 1179648

commit v9 on v8

--- a/solution.py
+++ b/solution.py
@@ -266,12 +266,12 @@
     across(1, 0)
     settle(0, 2)
     along(1, 2)
+    hand_on(0)
     across(1, 1)
-    hand_on(0)
+    hand_on(1)
     settle(1, 0)
-    hand_on(1)
+    hand_on(2)
     settle(1, 1)
-    hand_on(2)
     across(1, 2)
     multiply(0)
     multiply(1)

time: 55.9 us -> 55.9 us (level)
  no operation moved by 1% of the time
where the time goes in v9:
time: 55.9 us; the launch traced here: 55 us
  Pallas kernels  54.1 us (97%)
  local copies, waits for them, and re-layouts  0.82 us (1%)
    pallas_call x1, Pallas kernels, body(): pl.pallas_call(kernel, out_shape=pltpu.VMEM((KB, IB, WIDTH), BF16), in_sp...  54.1 us

profile of v9, /device:TPU:8, one launch (start us, length us, event | category | flops | bytes accessed | tf_op | source)
XLA Modules:
  0.0 55.0 jit_solution(8611840303505267113)
XLA Ops:
  0.0 54.1 %triangle.1 = bf16[96,24,128]{2,1,0:T(8,128)(2,1)S(1)} custom-call(bf16[96,24,128]{2,1,0:T(8,128)(2,1)} %x_hbm.1, f32[1,128]{1,0:T(1,128)} %bitcast.2, bf16[128,128]{1,0:T(8,128)(2,1)} %lw_hbm.1, bf16[128,128]{1,0:T(8,128)(2,1)} %rw_hbm.1, bf16[128,128]{1,0:T(8,128)(2,1)} %lg_hbm.1, bf16[128,128]{1,0:T(8,128)(2,1)} %rg_hbm.1, f32[1,128]{1,0:T(1,128)} %bitcast.3, ...), custom_call_target="tpu_custom_call" | custom-call | tf_op jit(solution)/shard_map/triangle/pallas_call | solution.py:355
  54.2 0.8 %copy.11 = bf16[96,24,128]{2,1,0:T(8,128)(2,1)} copy(bf16[96,24,128]{2,1,0:T(8,128)(2,1)S(1)} %triangle.1) | data formatting | bytes 1179648
